TPU v7x, 128 devices: a whole 4x4x4 slice. The times are simulated.
128 devices in a mesh: rep: 2 (over core), dp: 64 (over x, y, z).
Axes of the slice: x: 4, y: 4, z: 4, core: 2. Of those that a mesh axis runs over, the one named last changes fastest.
Arguments:
- x: bfloat16 [128, 2048, 1024], P(('rep', 'dp')), parts along dimension 0
- dy: bfloat16 [128, 2048, 1024], P(('rep', 'dp')), parts along dimension 0
- w_gate: bfloat16 [2, 1024, 6144], P(None, 'dp')
- w_up: bfloat16 [2, 1024, 6144], P(None, 'dp')
- w_down: bfloat16 [2, 6144, 1024], P(None, 'dp')
Outputs:
- output 1: bfloat16 [128, 2048, 1024], P(('rep', 'dp')), parts along dimension 0
- output 2: bfloat16 [4, 1024, 6144], P('rep', 'dp'), parts along dimension 0
- output 3: bfloat16 [4, 1024, 6144], P('rep', 'dp'), parts along dimension 0
- output 4: bfloat16 [4, 6144, 1024], P('rep', 'dp'), parts along dimension 0
There are 2 independent parts. A program takes and returns all parts, laid end to end along the dimension named above; an argument that names none is the same for every part.
All inputs are finite; a program needn't handle non-finite values.
Results may differ from a plain program's by a relative error of at most 0.018.
Values are sent between devices in bfloat16 or wider.
A program may use at most 1.5 GiB of HBM per device.

v0:
```python
import jax
import jax.numpy as jnp
from jax import lax

NAMES = ("w_gate", "w_up", "w_down")


def matmul(a, w):
    return jnp.dot(a, w, preferred_element_type=jnp.float32).astype(jnp.bfloat16)


def normed(h):
    wide = h.astype(jnp.float32)
    scale = lax.rsqrt(jnp.mean(wide**2, -1, keepdims=True) + 1e-6)
    return (wide * scale).astype(jnp.bfloat16)


def layer(h, w):
    a = normed(h)
    gate = jnp.dot(a, w["w_gate"], preferred_element_type=jnp.float32)
    up = jnp.dot(a, w["w_up"], preferred_element_type=jnp.float32)
    return h + matmul((jax.nn.silu(gate) * up).astype(jnp.bfloat16), w["w_down"])


def stack(weights, h):
    for number in range(weights["w_gate"].shape[0]):
        h = layer(h, {name: w[number] for name, w in weights.items()})
    return h


def solution(mesh):
    groups = mesh.shape["rep"]

    def step(x, dy, *weights):
        shape = x.shape
        x, dy = (t.reshape(groups, -1, *t.shape[1:]) for t in (x, dy))

        def of_a_group(x, dy):
            _, back = jax.vjp(stack, dict(zip(NAMES, weights, strict=True)), x)
            by_weights, by_x = back(dy)
            return (by_x, *(by_weights[name] for name in NAMES))

        by_x, *by_weights = jax.vmap(of_a_group)(x, dy)
        return (by_x.reshape(shape), *(t.reshape(-1, *t.shape[2:]) for t in by_weights))

    return step
```

profile of v0, /device:TPU:0, one launch (start us, length us, event | category | flops | bytes accessed | tf_op | source)
XLA Modules:
  0.0 2284.7 jit_solution(14476646510556959058)
XLA Ops:
  31.1 72.9 %all-gather.29.cloned.1.call-done = bf16[1,1024,6144]{2,1,0:T(8,128)(2,1)} async-done(((bf16[1,16,6144]{2,1,0:T(8,128)(2,1)}), bf16[1,1024,6144]{2,1,0:T(8,128)(2,1)}) %all-gather.29.cloned.1.call-update) | async-done | bytes 12582928 | tf_op jit(solution)/vmap(jvp())/squeeze | solution.py:27
  104.1 34.9 %fusion.57 = f32[2048,6144]{1,0:T(8,128)} fusion(bf16[1,1024,6144]{2,1,0:T(8,128)(2,1)} %all-gather.29.cloned.1.call-done, bf16[1,2048,1024]{2,1,0:T(8,128)(2,1)} %param.1, f32[2048]{0:T(1024)S(1)} %get-tuple-element.13), kind=kOutput, calls=%fused_computation.69 | convolution fusion | flops 25776095232 | bytes 67117056 | tf_op jit(solution)/vmap(jvp())/dot_general | solution.py:20
  139.0 58.8 %all-gather.31.cloned.1.call-done = bf16[1,1024,6144]{2,1,0:T(8,128)(2,1)} async-done(((bf16[1,16,6144]{2,1,0:T(8,128)(2,1)}), bf16[1,1024,6144]{2,1,0:T(8,128)(2,1)}) %all-gather.31.cloned.1.call-update) | async-done | bytes 12582928 | tf_op jit(solution)/vmap(jvp())/squeeze | solution.py:27
  197.8 34.9 %fusion.53 = f32[2048,6144]{1,0:T(8,128)} fusion(bf16[1,1024,6144]{2,1,0:T(8,128)(2,1)} %all-gather.31.cloned.1.call-done, bf16[1,2048,1024]{2,1,0:T(8,128)(2,1)} %param.1, f32[2048]{0:T(1024)S(1)} %get-tuple-element.13), kind=kOutput, calls=%fused_computation.65 | convolution fusion | flops 25776095232 | bytes 67117056 | tf_op jit(solution)/vmap(jvp())/dot_general | solution.py:21
  232.7 40.6 %fusion.24 = bf16[2048,6144]{1,0:T(8,128)(2,1)} fusion(f32[2048,6144]{1,0:T(8,128)} %fusion.53, f32[2048,6144]{1,0:T(8,128)} %fusion.57), kind=kLoop, calls=%fused_computation.34 | loop fusion | flops 75497472 | bytes 125829120
  273.3 17.7 all-gather.33.cloned.1.call-done
  291.0 46.6 %fusion.67 = (f32[2048]{0:T(1024)S(1)}, bf16[1,1,2048,1024]{2,3,1,0:T(8,128)(2,1)}) fusion(bf16[2048,6144]{1,0:T(8,128)(2,1)} %fusion.24, bf16[1,6144,1024]{2,1,0:T(8,128)(2,1)} %all-gather.33.cloned.1.call-done, bf16[1,2048,1024]{1,2,0:T(8,128)(2,1)} %copy.1), kind=kOutput, calls=%fused_computation.86 | convolution fusion | flops 25780287488 | bytes 46145536 | tf_op jit(solution)/vmap(jvp())/dot_general | solution.py:9
  338.2 46.4 %all-gather.35.cloned.1.call-done = bf16[1,1024,6144]{2,1,0:T(8,128)(2,1)} async-done(((bf16[1,16,6144]{2,1,0:T(8,128)(2,1)}), bf16[1,1024,6144]{2,1,0:T(8,128)(2,1)}) %all-gather.35.cloned.1.call-update) | async-done | bytes 12582928 | tf_op jit(solution)/vmap(jvp())/squeeze | solution.py:27
  384.5 35.0 %fusion.47 = f32[2048,6144]{1,0:T(8,128)} fusion(bf16[1,1024,6144]{2,1,0:T(8,128)(2,1)} %all-gather.35.cloned.1.call-done, bf16[1,1,2048,1024]{2,3,1,0:T(8,128)(2,1)} %get-tuple-element.15, f32[2048]{0:T(1024)S(1)} %bitcast.291), kind=kOutput, calls=%fused_computation.59 | convolution fusion | flops 25776095232 | bytes 67117056 | tf_op jit(solution)/vmap(jvp())/dot_general | solution.py:20
  419.6 58.5 %all-gather.39.cloned.1.call-done = bf16[1,1024,6144]{2,1,0:T(8,128)(2,1)} async-done(((bf16[1,16,6144]{2,1,0:T(8,128)(2,1)}), bf16[1,1024,6144]{2,1,0:T(8,128)(2,1)}) %all-gather.39.cloned.1.call-update) | async-done | bytes 12582928 | tf_op jit(solution)/vmap(jvp())/squeeze | solution.py:27
  478.1 35.0 %fusion.41 = f32[2048,6144]{1,0:T(8,128)} fusion(bf16[1,1024,6144]{2,1,0:T(8,128)(2,1)} %all-gather.39.cloned.1.call-done, bf16[1,1,2048,1024]{2,3,1,0:T(8,128)(2,1)} %get-tuple-element.15, f32[2048]{0:T(1024)S(1)} %bitcast.292), kind=kOutput, calls=%fused_computation.53 | convolution fusion | flops 25776095232 | bytes 67117056 | tf_op jit(solution)/vmap(jvp())/dot_general | solution.py:21
  513.1 58.0 %all-gather.37.cloned.1.call-done = bf16[1,6144,1024]{2,1,0:T(8,128)(2,1)} async-done(((bf16[1,96,1024]{2,1,0:T(8,128)(2,1)}), bf16[1,6144,1024]{2,1,0:T(8,128)(2,1)}) %all-gather.37.cloned.1.call-update) | async-done | bytes 12582928 | tf_op jit(solution)/vmap(jvp())/squeeze | solution.py:27
  571.1 33.9 %convolution_convert_fusion.1 = bf16[2048,6144]{1,0:T(8,128)(2,1)} fusion(bf16[1,6144,1024]{2,1,0:T(8,128)(2,1)} %all-gather.37.cloned.1.call-done, bf16[1,2048,1024]{2,1,0:T(8,128)(2,1)} %param), kind=kOutput, calls=%fused_computation.42 | convolution fusion | flops 25782386688 | bytes 41943040 | tf_op jit(solution)/vmap(transpose(jvp()))/dot_general | solution.py:9
  605.0 47.9 %fusion.4 = bf16[2048,6144]{1,0:T(8,128)(2,1)} fusion(f32[2048,6144]{1,0:T(8,128)} %fusion.47, f32[2048,6144]{1,0:T(8,128)} %fusion.41, bf16[2048,6144]{1,0:T(8,128)(2,1)} %convolution_convert_fusion.1), kind=kLoop, calls=%fused_computation.10 | loop fusion | flops 150994944 | bytes 150994944
  652.9 34.9 %fusion.45 = bf16[2048,1024]{0,1:T(8,128)(2,1)} fusion(bf16[2048,6144]{1,0:T(8,128)(2,1)} %fusion.4, bf16[1,1024,6144]{2,1,0:T(8,128)(2,1)} %all-gather.35.cloned.1.call-done), kind=kOutput, calls=%fused_computation.57 | convolution fusion | flops 25769803776 | bytes 41943040 | tf_op jit(solution)/vmap(transpose(jvp()))/dot_general | solution.py:20
  687.8 41.0 %fusion.69 = (f32[2048]{0:T(1024)S(1)}, bf16[2048,1024]{0,1:T(8,128)(2,1)}) fusion(bf16[1,1,2048,1024]{2,3,1,0:T(8,128)(2,1)S(1)} %copy-done.3, bf16[2048,1024]{0,1:T(8,128)(2,1)} %fusion.45, bf16[1,1024,6144]{2,1,0:T(8,128)(2,1)} %all-gather.39.cloned.1.call-done, bf16[2048,6144]{1,0:T(8,128)(2,1)} %convolution_convert_fusion.1, f32[2048,6144]{1,0:T(8,128)} %fusion.47), kind=kOutput, calls=%fused_computation.88 | convolution fusion | flops 25857882112 | bytes 100671488 | tf_op jit(solution)/vmap(transpose(jvp()))/dot_general | solution.py:21
  735.6 31.6 %convolution_bitcast_fusion = f32[1,6144,1024]{2,1,0:T(8,128)} fusion(bf16[2048,6144]{1,0:T(8,128)(2,1)} %fusion.24, bf16[1,1,2048,1024]{2,3,1,0:T(8,128)(2,1)S(1)} %fusion.74), kind=kOutput, calls=%fused_computation.47 | convolution fusion | flops 25769803776 | bytes 54525952 | tf_op jit(solution)/vmap(transpose(jvp()))/dot_general | solution.py:9
  767.3 45.8 %fusion.32 = f32[1,6144,1024]{2,1,0:T(8,128)} fusion(f32[2048,6144]{1,0:T(8,128)} %fusion.41, f32[2048,6144]{1,0:T(8,128)} %fusion.47, bf16[1,2048,1024]{2,1,0:T(8,128)(2,1)} %param), kind=kOutput, calls=%fused_computation.48 | convolution fusion | flops 25845301248 | bytes 130023424 | tf_op jit(solution)/vmap(transpose(jvp()))/dot_general | solution.py:9
  813.8 41.9 %fusion.35 = f32[1,1024,6144]{2,1,0:T(8,128)} fusion(bf16[2048,6144]{1,0:T(8,128)(2,1)} %convolution_convert_fusion.1, f32[2048,6144]{1,0:T(8,128)} %fusion.47, bf16[1,1,2048,1024]{2,3,1,0:T(8,128)(2,1)} %get-tuple-element.15, f32[2048]{0:T(1024)S(1)} %bitcast.294), kind=kOutput, calls=%fused_computation.51 | convolution fusion | flops 25851592704 | bytes 104865792 | tf_op jit(solution)/vmap(transpose(jvp()))/dot_general | solution.py:21
  855.8 34.1 %convolution_convert_fusion = bf16[2048,6144]{1,0:T(8,128)(2,1)} fusion(bf16[1,6144,1024]{2,1,0:T(8,128)(2,1)} %all-gather.33.cloned.1.call-done, bf16[1,1,2048,1024]{2,3,1,0:T(8,128)(2,1)} %copy-done), kind=kOutput, calls=%fused_computation.41 | convolution fusion | flops 25782386688 | bytes 41943040 | tf_op jit(solution)/vmap(transpose(jvp()))/dot_general | solution.py:9
  889.9 47.9 %fusion.7 = bf16[2048,6144]{1,0:T(8,128)(2,1)} fusion(f32[2048,6144]{1,0:T(8,128)} %fusion.57, f32[2048,6144]{1,0:T(8,128)} %fusion.53, bf16[2048,6144]{1,0:T(8,128)(2,1)} %convolution_convert_fusion), kind=kLoop, calls=%fused_computation.13 | loop fusion | flops 150994944 | bytes 150994944
  937.8 33.7 %fusion.55 = bf16[2048,1024]{0,1:T(8,128)(2,1)S(1)} fusion(bf16[2048,6144]{1,0:T(8,128)(2,1)} %fusion.7, bf16[1,1024,6144]{2,1,0:T(8,128)(2,1)} %all-gather.29.cloned.1.call-done), kind=kOutput, calls=%fused_computation.67 | convolution fusion | flops 25769803776 | bytes 41943040 | tf_op jit(solution)/vmap(transpose(jvp()))/dot_general | solution.py:20
  971.6 37.8 %fusion.65 = (f32[2048]{0:T(1024)S(1)}, bf16[2048,1024]{0,1:T(8,128)(2,1)}) fusion(bf16[1,2048,1024]{1,2,0:T(8,128)(2,1)S(1)} %copy-done.1, bf16[2048,1024]{0,1:T(8,128)(2,1)S(1)} %fusion.55, bf16[1,1024,6144]{2,1,0:T(8,128)(2,1)} %all-gather.31.cloned.1.call-done, bf16[2048,6144]{1,0:T(8,128)(2,1)} %convolution_convert_fusion, f32[2048,6144]{1,0:T(8,128)} %fusion.57), kind=kOutput, calls=%fused_computation.84 | convolution fusion | flops 25857882112 | bytes 100671488 | tf_op jit(solution)/vmap(transpose(jvp()))/dot_general | solution.py:21
  1010.0 42.1 %fusion.38 = f32[1,1024,6144]{2,1,0:T(8,128)} fusion(bf16[2048,6144]{1,0:T(8,128)(2,1)} %convolution_convert_fusion, f32[2048,6144]{1,0:T(8,128)} %fusion.57, bf16[1,2048,1024]{1,2,0:T(8,128)(2,1)} %copy.1, f32[2048]{0:T(1024)S(1)} %bitcast.296), kind=kOutput, calls=%fused_computation.52 | convolution fusion | flops 25851592704 | bytes 104865792 | tf_op jit(solution)/vmap(transpose(jvp()))/dot_general | solution.py:21
  1052.8 32.5 %convolution_bitcast_fusion.2 = f32[1,1024,6144]{2,1,0:T(8,128)} fusion(bf16[2048,6144]{1,0:T(8,128)(2,1)} %fusion.4, bf16[1,1,2048,1024]{2,3,1,0:T(8,128)(2,1)} %get-tuple-element.15, f32[2048]{0:T(1024)S(1)} %bitcast.295), kind=kOutput, calls=%fused_computation.50 | convolution fusion | flops 25776095232 | bytes 54534144 | tf_op jit(solution)/vmap(transpose(jvp()))/dot_general | solution.py:20
  1085.4 32.8 %convolution_bitcast_fusion.1 = f32[1,1024,6144]{2,1,0:T(8,128)} fusion(bf16[2048,6144]{1,0:T(8,128)(2,1)} %fusion.7, bf16[1,2048,1024]{1,2,0:T(8,128)(2,1)} %copy.1, f32[2048]{0:T(1024)S(1)} %bitcast.297), kind=kOutput, calls=%fused_computation.49 | convolution fusion | flops 25776095232 | bytes 54534144 | tf_op jit(solution)/vmap(transpose(jvp()))/dot_general | solution.py:20
  1118.9 7.7 fusion.73
  1134.0 135.0 %reduce-scatter.27.cloned.1.call-done = f32[1,96,1024]{2,1,0:T(8,128)} async-done(((f32[1,6144,1024]{2,1,0:T(8,128)}), f32[1,96,1024]{2,1,0:T(8,128)}) %reduce-scatter.27.cloned.1.call-update) | async-done | bytes 393232
  1270.7 250.3 %reduce-scatter.23.cloned.1.call-done = f32[1,16,6144]{2,1,0:T(8,128)} async-done(((f32[1,1024,6144]{2,1,0:T(8,128)}), f32[1,16,6144]{2,1,0:T(8,128)}) %reduce-scatter.23.cloned.1.call-update) | async-done | bytes 393232
  1522.1 250.7 %reduce-scatter.25.cloned.1.call-done = f32[1,16,6144]{2,1,0:T(8,128)} async-done(((f32[1,1024,6144]{2,1,0:T(8,128)}), f32[1,16,6144]{2,1,0:T(8,128)}) %reduce-scatter.25.cloned.1.call-update) | async-done | bytes 393232
  1774.5 249.8 %reduce-scatter.19.cloned.1.call-done = f32[1,16,6144]{2,1,0:T(8,128)} async-done(((f32[1,1024,6144]{2,1,0:T(8,128)}), f32[1,16,6144]{2,1,0:T(8,128)}) %reduce-scatter.19.cloned.1.call-update) | async-done | bytes 393232
  2025.4 250.5 %reduce-scatter.21.cloned.1.call-done = f32[1,16,6144]{2,1,0:T(8,128)} async-done(((f32[1,1024,6144]{2,1,0:T(8,128)}), f32[1,16,6144]{2,1,0:T(8,128)}) %reduce-scatter.21.cloned.1.call-update) | async-done | bytes 393232
  (71 shorter events, 48.9 us)
Async XLA Ops:
  7.2 96.9 %all-gather.29.cloned.1.call-start = ((), (), s32[]{:S(2)}) async-start(), calls=%async_computation.6 | async-start | bytes 12779520 | tf_op jit(solution)/vmap(jvp())/squeeze | solution.py:27
  9.0 188.8 %all-gather.31.cloned.1.call-start = ((), (), s32[]{:S(2)}) async-start(), calls=%async_computation.7 | async-start | bytes 12779520 | tf_op jit(solution)/vmap(jvp())/squeeze | solution.py:27
  10.9 280.1 %all-gather.33.cloned.1.call-start = ((), (), s32[]{:S(2)}) async-start(), calls=%async_computation.8 | async-start | bytes 12779520 | tf_op jit(solution)/vmap(jvp())/squeeze | solution.py:27
  12.7 371.8 %all-gather.35.cloned.1.call-start = ((), (), s32[]{:S(2)}) async-start(), calls=%async_computation.9 | async-start | bytes 12779520 | tf_op jit(solution)/vmap(jvp())/squeeze | solution.py:27
  13.3 464.8 %all-gather.39.cloned.1.call-start = ((), (), s32[]{:S(2)}) async-start(), calls=%async_computation.11 | async-start | bytes 12779520 | tf_op jit(solution)/vmap(jvp())/squeeze | solution.py:27
  13.9 557.2 %all-gather.37.cloned.1.call-start = ((), (), s32[]{:S(2)}) async-start(), calls=%async_computation.10 | async-start | bytes 12779520 | tf_op jit(solution)/vmap(jvp())/squeeze | solution.py:27
  14.5 1118.5 %reduce-scatter.29.cloned.1.call-start = ((), (), s32[]{:S(2)}) async-start(), calls=%async_computation.17 | async-start | bytes 25559040
  337.5 0.6 copy-start.4
  338.2 140.0 %copy-start.6 = (f32[1,1,2048]{2,1,0:T(1,128)}, f32[1,1,2048]{2,1,0:T(1,128)S(1)}, u32[]{:S(2)}) copy-start(f32[1,1,2048]{2,1,0:T(1,128)S(1)} %rsqrt.23) | copy-start | bytes 24580
  652.9 34.9 %copy-start.3 = (bf16[1,1,2048,1024]{2,3,1,0:T(8,128)(2,1)S(1)}, bf16[1,1,2048,1024]{2,3,1,0:T(8,128)(2,1)}, u32[]{:S(2)}) copy-start(bf16[1,1,2048,1024]{2,3,1,0:T(8,128)(2,1)} %get-tuple-element.15) | copy-start | bytes 12582916
  687.8 41.0 %copy-start.5 = (f32[2048]{0:T(1024)S(1)}, f32[2048]{0:T(1024)}, u32[]{:S(2)}) copy-start(f32[2048]{0:T(1024)} %copy-done.4) | copy-start | bytes 24580
  687.8 41.0 %copy-start.2 = (bf16[1,2048,1024]{1,2,0:T(8,128)(2,1)S(1)}, bf16[1,2048,1024]{1,2,0:T(8,128)(2,1)}, u32[]{:S(2)}) copy-start(bf16[1,2048,1024]{1,2,0:T(8,128)(2,1)} %copy) | copy-start | bytes 12582916
  687.8 41.0 %copy-start.7 = (f32[1,1,2048]{2,1,0:T(1,128)S(1)}, f32[1,1,2048]{2,1,0:T(1,128)}, u32[]{:S(2)}) copy-start(f32[1,1,2048]{2,1,0:T(1,128)} %copy-done.6) | copy-start | bytes 24580
  733.6 2.0 copy-start
  767.2 501.7 %reduce-scatter.27.cloned.1.call-start = ((), (), s32[]{:S(2)}) async-start(), calls=%async_computation.16 | async-start | bytes 25559040
  813.1 0.7 copy-start.8
  813.1 707.9 %reduce-scatter.23.cloned.1.call-start = ((), (), s32[]{:S(2)}) async-start(), calls=%async_computation.14 | async-start | bytes 25559040
  855.8 917.0 %reduce-scatter.25.cloned.1.call-start = ((), (), s32[]{:S(2)}) async-start(), calls=%async_computation.15 | async-start | bytes 25559040
  937.8 33.7 %copy-start.1 = (bf16[1,2048,1024]{1,2,0:T(8,128)(2,1)S(1)}, bf16[1,2048,1024]{1,2,0:T(8,128)(2,1)}, u32[]{:S(2)}) copy-start(bf16[1,2048,1024]{1,2,0:T(8,128)(2,1)} %copy.1) | copy-start | bytes 12582916
  971.6 37.8 %copy-start.11 = (f32[2048]{0:T(1024)S(1)}, f32[2048]{0:T(1024)}, u32[]{:S(2)}) copy-start(f32[2048]{0:T(1024)} %get-tuple-element.12) | copy-start | bytes 24580
  1052.1 0.7 copy-start.9
  1052.1 972.2 %reduce-scatter.19.cloned.1.call-start = ((), (), s32[]{:S(2)}) async-start(), calls=%async_computation.12 | async-start | bytes 25559040
  1085.3 1190.5 %reduce-scatter.21.cloned.1.call-start = ((), (), s32[]{:S(2)}) async-start(), calls=%async_computation.13 | async-start | bytes 25559040
  1118.2 0.7 copy-start.10
Sparse Core Ops, SparseCore 0:
  10.8 93.2 all-gather.28
  107.5 90.2 all-gather.30
  200.7 90.2 all-gather.32
  294.2 90.2 all-gather.34
  387.8 90.2 all-gather.38
  480.8 90.2 all-gather.36
  767.4 249.5 reduce-scatter.28
  1021.6 247.2 reduce-scatter.26
  1273.6 247.3 reduce-scatter.22
  1525.6 247.0 reduce-scatter.24
  1777.4 246.8 reduce-scatter.18
  2028.9 246.8 reduce-scatter.20
where the time goes:
time: 2300 us; the launch traced here: 2280 us
  waiting for transfers between devices  1450 us (63%)
  matrix products  629 us (27%)
  other arithmetic  162 us (7%)
  local copies, waits for them, and re-layouts  29.2 us (1%)
    unnamed x18, waiting for transfers between devices  1140 us
    squeeze x6, waiting for transfers between devices, stack(): h = layer(h, {name: w[number] for name, w in weights.items()})  312 us
    dot_general x6, matrix products, layer(): up = jnp.dot(a, w['w_up'], preferred_element_type=jnp.float32)  233 us
    dot_general x6, matrix products, layer(): gate = jnp.dot(a, w['w_gate'], preferred_element_type=jnp.float32)  204 us
    dot_general x5, matrix products, matmul(): jnp.dot(a, w, preferred_element_type=jnp.float32).astype(jnp.bfloat16)  192 us
    unnamed x3, other arithmetic  136 us
  transfers between devices with their start and end apart: 12, of which 11 were waited for; matrix products, arithmetic and copies ran while one was open for 27% of the time, Pallas kernels for 0%

commit v1 on v0

v1 whole, which is shorter than its diff:
```python
import jax
import jax.numpy as jnp
from jax import lax
from jax.sharding import PartitionSpec as P

BF, F32 = jnp.bfloat16, jnp.float32
LAYERS = 2


def dot(a, b, dims):
    return lax.dot_general(a, b, (dims, ((), ())), preferred_element_type=F32)


def gather(w):
    half = w.shape[0] // 2
    mine = lax.dynamic_slice_in_dim(w, lax.axis_index("rep") * half, half, 0)
    return lax.all_gather(mine, ("dp", "rep"), axis=0, tiled=True)


def scatter(term):
    return lax.psum_scatter(term.astype(BF), "dp", scatter_dimension=0, tiled=True)


def scale_of(h):
    wide = h.astype(F32)
    return lax.rsqrt(jnp.mean(wide * wide, -1, keepdims=True) + 1e-6)


def body(x, dy, w_gate, w_up, w_down):
    h, g = x[0], dy[0]
    weights = [[gather(w[n]) for w in (w_gate, w_up, w_down)] for n in range(LAYERS)]
    saved = []
    for n in range(LAYERS):
        wg, wu, wd = weights[n]
        s = scale_of(h)
        a = (h.astype(F32) * s).astype(BF)
        gate = dot(a, wg, ((1,), (0,)))
        up = dot(a, wu, ((1,), (0,)))
        hid = (jax.nn.silu(gate) * up).astype(BF)
        saved.append((h, s, a, gate, up, hid))
        if n < LAYERS - 1:
            h = h + dot(hid, wd, ((1,), (0,))).astype(BF)
    grads = [None] * LAYERS
    for n in reversed(range(LAYERS)):
        wg, wu, wd = weights[n]
        h, s, a, gate, up, hid = saved[n]
        d_wd = scatter(dot(hid, g, ((0,), (0,))))
        d_hid = dot(g, wd, ((1,), (1,))).astype(BF).astype(F32)
        sig = jax.nn.sigmoid(gate)
        d_gate = (d_hid * up * (sig * (1 + gate * (1 - sig)))).astype(BF)
        d_up = (d_hid * (gate * sig)).astype(BF)
        d_wg = scatter(dot(a, d_gate, ((0,), (0,))))
        d_wu = scatter(dot(a, d_up, ((0,), (0,))))
        d_a = (dot(d_gate, wg, ((1,), (1,))) + dot(d_up, wu, ((1,), (1,)))).astype(BF).astype(F32)
        wide = h.astype(F32)
        inner = jnp.sum(d_a * wide, -1, keepdims=True) * (s * s * s / h.shape[-1])
        g = g + (d_a * s - wide * inner).astype(BF)
        grads[n] = (d_wg, d_wu, d_wd)
    return (g[None], *(jnp.stack(t) for t in zip(*grads)))


def solution(mesh):
    seq, row = P(("rep", "dp")), P(None, "dp")
    out = P("rep", "dp")
    return jax.shard_map(body, mesh=mesh, in_specs=(seq, seq, row, row, row), out_specs=(seq, out, out, out), check_vma=False)
```

time: 2300 us -> 2060 us (0.90)
  other arithmetic: 162 us -> 17.9 us
  waiting for transfers between devices: 1450 us -> 1320 us
  matrix products: 629 us -> 674 us
    unnamed x18 -> x12, waiting for transfers between devices: 1140 us -> 0.2 us
    reduce_scatter x0 -> x6, waiting for transfers between devices: none -> 1080 us  [scatter(): lax.psum_scatter(term.astype(BF), 'dp', scatter_dimension=0, tiled=True)]
    squeeze x6 -> x0, waiting for transfers between devices: 312 us -> none  [stack(): h = layer(h, {name: w[number] for name, w in weights.items()})]
    all_gather x0 -> x6, waiting for transfers between devices: none -> 236 us  [gather(): return lax.all_gather(mine, ('dp', 'rep'), axis=0, tiled=True)]
    unnamed x3 -> x0, other arithmetic: 136 us -> none
    dot_general x17, matrix products: 629 us -> 674 us  [dot(): return lax.dot_general(a, b, (dims, ((), ())), preferred_element_type=F32)]
  transfers between devices with their start and end apart: 12 -> 12, of which waited for: 11 -> 11; matrix products, arithmetic and copies ran while one was open for 27% -> 26% of each run, Pallas kernels for 0% -> 0%
where the time goes in v1:
time: 2060 us; the launch traced here: 2050 us
  waiting for transfers between devices  1320 us (64%)
  matrix products  674 us (33%)
  local copies, waits for them, and re-layouts  30.3 us (1%)
    reduce_scatter x6, waiting for transfers between devices, scatter(): lax.psum_scatter(term.astype(BF), 'dp', scatter_dimension=0, tiled=True)  1080 us
    dot_general x17, matrix products, dot(): return lax.dot_general(a, b, (dims, ((), ())), preferred_element_type=F32)  674 us
    all_gather x6, waiting for transfers between devices, gather(): return lax.all_gather(mine, ('dp', 'rep'), axis=0, tiled=True)  236 us
  transfers between devices with their start and end apart: 12, of which 11 were waited for; matrix products, arithmetic and copies ran while one was open for 26% of the time, Pallas kernels for 0%

profile of v1, /device:TPU:0, one launch (start us, length us, event | category | flops | bytes accessed | tf_op | source)
XLA Modules:
  0.0 2053.5 jit_solution(7053796805725095040)
XLA Ops:
  14.7 6.4 copy.10
  24.9 6.6 copy.9
  31.4 55.4 %all-gather.15.cloned.1.call-done = bf16[1,1024,6144]{2,1,0:T(8,128)(2,1)} async-done(((bf16[1,8,6144]{2,1,0:T(8,128)(2,1)}), bf16[1,1024,6144]{2,1,0:T(8,128)(2,1)}) %all-gather.15.cloned.1.call-update) | async-done | bytes 12582928 | tf_op jit(solution)/shard_map/all_gather | solution.py:17
  86.9 34.7 %fusion.26 = f32[2048,6144]{0,1:T(8,128)} fusion(bf16[1,1024,6144]{2,1,0:T(8,128)(2,1)} %all-gather.15.cloned.1.call-done, bf16[1,2048,1024]{1,2,0:T(8,128)(2,1)} %copy.10, f32[2048]{0:T(1024)S(1)} %add_rsqrt_fusion.1), kind=kOutput, calls=%fused_computation.44 | convolution fusion | flops 25776095232 | bytes 67117056 | tf_op jit(solution)/shard_map/dot_general | solution.py:11
  121.5 41.1 %all-gather.17.cloned.1.call-done = bf16[1,1024,6144]{2,1,0:T(8,128)(2,1)} async-done(((bf16[1,8,6144]{2,1,0:T(8,128)(2,1)}), bf16[1,1024,6144]{2,1,0:T(8,128)(2,1)}) %all-gather.17.cloned.1.call-update) | async-done | bytes 12582928 | tf_op jit(solution)/shard_map/all_gather | solution.py:17
  162.7 56.6 %multiply_convert_fusion.1 = (bf16[2048,6144]{0,1:T(8,128)(2,1)}, f32[2048,6144]{0,1:T(8,128)}) fusion(f32[2048,6144]{0,1:T(8,128)} %fusion.26, bf16[1,1024,6144]{2,1,0:T(8,128)(2,1)} %all-gather.17.cloned.1.call-done, bf16[1,2048,1024]{1,2,0:T(8,128)(2,1)} %copy.10, f32[2048]{0:T(1024)S(1)} %add_rsqrt_fusion.1), kind=kOutput, calls=%fused_computation.13 | convolution fusion | flops 25851592704 | bytes 142614528 | tf_op jit(solution)/shard_map/dot_general | solution.py:11
  219.2 19.3 all-gather.19.cloned.1.call-done
  238.5 35.2 %fusion.38 = (f32[2048]{0:T(1024)S(1)}, bf16[2048,1024]{0,1:T(8,128)(2,1)}) fusion(bf16[2048,6144]{0,1:T(8,128)(2,1)} %get-tuple-element.18, bf16[1,6144,1024]{2,1,0:T(8,128)(2,1)} %all-gather.19.cloned.1.call-done, bf16[1,2048,1024]{1,2,0:T(8,128)(2,1)} %copy.10), kind=kOutput, calls=%fused_computation.62 | convolution fusion | flops 25780287488 | bytes 46145536 | tf_op jit(solution)/shard_map/dot_general | solution.py:11
  273.7 39.9 %all-gather.21.cloned.1.call-done = bf16[1,1024,6144]{2,1,0:T(8,128)(2,1)} async-done(((bf16[1,8,6144]{2,1,0:T(8,128)(2,1)}), bf16[1,1024,6144]{2,1,0:T(8,128)(2,1)}) %all-gather.21.cloned.1.call-update) | async-done | bytes 12582928 | tf_op jit(solution)/shard_map/all_gather | solution.py:17
  313.6 35.2 %fusion.15 = f32[2048,6144]{0,1:T(8,128)} fusion(bf16[1,1024,6144]{2,1,0:T(8,128)(2,1)} %all-gather.21.cloned.1.call-done, bf16[2048,1024]{0,1:T(8,128)(2,1)} %get-tuple-element.21, f32[2048]{0:T(1024)S(1)} %add_rsqrt_fusion), kind=kOutput, calls=%fused_computation.33 | convolution fusion | flops 25776095232 | bytes 67117056 | tf_op jit(solution)/shard_map/dot_general | solution.py:11
  348.8 39.9 %all-gather.23.cloned.1.call-done = bf16[1,1024,6144]{2,1,0:T(8,128)(2,1)} async-done(((bf16[1,8,6144]{2,1,0:T(8,128)(2,1)}), bf16[1,1024,6144]{2,1,0:T(8,128)(2,1)}) %all-gather.23.cloned.1.call-update) | async-done | bytes 12582928 | tf_op jit(solution)/shard_map/all_gather | solution.py:17
  388.7 34.9 %fusion.11 = f32[2048,6144]{0,1:T(8,128)} fusion(bf16[1,1024,6144]{2,1,0:T(8,128)(2,1)} %all-gather.23.cloned.1.call-done, bf16[2048,1024]{0,1:T(8,128)(2,1)} %get-tuple-element.21, f32[2048]{0:T(1024)S(1)} %add_rsqrt_fusion), kind=kOutput, calls=%fused_computation.29 | convolution fusion | flops 25776095232 | bytes 67117056 | tf_op jit(solution)/shard_map/dot_general | solution.py:11
  423.6 40.2 %all-gather.13.cloned.1.call-done = bf16[1,6144,1024]{2,1,0:T(8,128)(2,1)} async-done(((bf16[1,48,1024]{2,1,0:T(8,128)(2,1)}), bf16[1,6144,1024]{2,1,0:T(8,128)(2,1)}) %all-gather.13.cloned.1.call-update) | async-done | bytes 12582928 | tf_op jit(solution)/shard_map/all_gather | solution.py:17
  463.8 65.9 %fusion.5 = (bf16[2048,6144]{0,1:T(8,128)(2,1)}, bf16[2048,6144]{0,1:T(8,128)(2,1)}) fusion(f32[2048,6144]{0,1:T(8,128)} %fusion.11, f32[2048,6144]{0,1:T(8,128)} %fusion.15, bf16[1,2048,1024]{2,1,0:T(8,128)(2,1)} %param.6, bf16[1,6144,1024]{2,1,0:T(8,128)(2,1)} %all-gather.13.cloned.1.call-done), kind=kOutput, calls=%fused_computation.9 | convolution fusion | flops 25958547456 | bytes 167772160 | tf_op jit(solution)/shard_map/dot_general | solution.py:11
  529.7 34.8 %fusion.9 = f32[2048,1024]{0,1:T(8,128)} fusion(bf16[2048,6144]{0,1:T(8,128)(2,1)} %get-tuple-element.11, bf16[1,1024,6144]{2,1,0:T(8,128)(2,1)} %all-gather.23.cloned.1.call-done), kind=kOutput, calls=%fused_computation.27 | convolution fusion | flops 25769803776 | bytes 46137344 | tf_op jit(solution)/shard_map/dot_general | solution.py:11
  564.5 35.2 %fusion.40 = (f32[2048]{0:T(1024)S(1)}, bf16[2048,1024]{0,1:T(8,128)(2,1)}) fusion(bf16[2048,1024]{0,1:T(8,128)(2,1)S(1)} %copy-done.4, f32[2048,1024]{0,1:T(8,128)} %fusion.9, bf16[2048,6144]{0,1:T(8,128)(2,1)} %get-tuple-element.10, bf16[1,1024,6144]{2,1,0:T(8,128)(2,1)} %all-gather.21.cloned.1.call-done), kind=kOutput, calls=%fused_computation.64 | convolution fusion | flops 25782384640 | bytes 54534144 | tf_op jit(solution)/shard_map/dot_general | solution.py:11
  599.7 4.7 fusion.43
  606.4 32.0 %convolution_convert_fusion.2 = bf16[6144,1024]{1,0:T(8,128)(2,1)} fusion(bf16[2048,6144]{0,1:T(8,128)(2,1)} %get-tuple-element.18, bf16[2048,1024]{0,1:T(8,128)(2,1)S(1)} %fusion.43), kind=kOutput, calls=%fused_computation.47 | convolution fusion | flops 25776095232 | bytes 41943040 | tf_op jit(solution)/shard_map/dot_general | solution.py:11
  638.5 43.4 %fusion.29 = bf16[6144,1024]{1,0:T(8,128)(2,1)} fusion(f32[2048,6144]{0,1:T(8,128)} %fusion.15, f32[2048,6144]{0,1:T(8,128)} %fusion.11, bf16[1,2048,1024]{2,1,0:T(8,128)(2,1)} %param.6), kind=kOutput, calls=%fused_computation.52 | convolution fusion | flops 25851592704 | bytes 117440512 | tf_op jit(solution)/shard_map/dot_general | solution.py:11
  682.6 32.8 %convolution_convert_fusion.3 = bf16[1024,6144]{1,0:T(8,128)(2,1)} fusion(bf16[2048,6144]{0,1:T(8,128)(2,1)} %get-tuple-element.10, bf16[2048,1024]{0,1:T(8,128)(2,1)} %get-tuple-element.21, f32[2048]{0:T(1024)S(1)} %copy-done.11), kind=kOutput, calls=%fused_computation.48 | convolution fusion | flops 25782386688 | bytes 41951232 | tf_op jit(solution)/shard_map/dot_general | solution.py:11
  715.4 66.6 %fusion.1 = (bf16[2048,6144]{0,1:T(8,128)(2,1)}, bf16[2048,6144]{0,1:T(8,128)(2,1)}) fusion(f32[2048,6144]{0,1:T(8,128)} %get-tuple-element.19, f32[2048,6144]{0,1:T(8,128)} %fusion.26, bf16[2048,1024]{0,1:T(8,128)(2,1)} %copy-done.1, bf16[1,6144,1024]{2,1,0:T(8,128)(2,1)} %all-gather.19.cloned.1.call-done), kind=kOutput, calls=%fused_computation.3 | convolution fusion | flops 25958547456 | bytes 167772160 | tf_op jit(solution)/shard_map/dot_general | solution.py:11
  782.0 32.6 %convolution_convert_fusion.4 = bf16[1024,6144]{1,0:T(8,128)(2,1)} fusion(bf16[2048,6144]{0,1:T(8,128)(2,1)} %get-tuple-element.9, bf16[1,2048,1024]{1,2,0:T(8,128)(2,1)} %copy.10, f32[2048]{0:T(1024)S(1)} %copy-done.8), kind=kOutput, calls=%fused_computation.49 | convolution fusion | flops 25782386688 | bytes 41951232 | tf_op jit(solution)/shard_map/dot_general | solution.py:11
  815.3 32.8 %convolution_convert_fusion.5 = bf16[1024,6144]{1,0:T(8,128)(2,1)} fusion(bf16[2048,6144]{0,1:T(8,128)(2,1)} %get-tuple-element.11, bf16[2048,1024]{0,1:T(8,128)(2,1)} %get-tuple-element.21, f32[2048]{0:T(1024)S(1)} %copy-done.12), kind=kOutput, calls=%fused_computation.50 | convolution fusion | flops 25782386688 | bytes 41951232 | tf_op jit(solution)/shard_map/dot_general | solution.py:11
  848.1 32.7 %convolution_convert_fusion.6 = bf16[1024,6144]{1,0:T(8,128)(2,1)} fusion(bf16[2048,6144]{0,1:T(8,128)(2,1)} %get-tuple-element.8, bf16[1,2048,1024]{1,2,0:T(8,128)(2,1)} %copy.10, f32[2048]{0:T(1024)S(1)} %copy-done.8), kind=kOutput, calls=%fused_computation.51 | convolution fusion | flops 25782386688 | bytes 41951232 | tf_op jit(solution)/shard_map/dot_general | solution.py:11
  880.8 34.6 %fusion.20 = f32[2048,1024]{0,1:T(8,128)} fusion(bf16[2048,6144]{0,1:T(8,128)(2,1)} %get-tuple-element.9, bf16[1,1024,6144]{2,1,0:T(8,128)(2,1)} %all-gather.17.cloned.1.call-done), kind=kOutput, calls=%fused_computation.38 | convolution fusion | flops 25769803776 | bytes 46137344 | tf_op jit(solution)/shard_map/dot_general | solution.py:11
  915.5 34.6 %fusion.37 = (f32[2048]{0:T(1024)S(1)}, bf16[2048,1024]{0,1:T(8,128)(2,1)S(1)}) fusion(bf16[1,2048,1024]{1,2,0:T(8,128)(2,1)S(1)} %copy-done, f32[2048,1024]{0,1:T(8,128)} %fusion.20, bf16[2048,6144]{0,1:T(8,128)(2,1)} %get-tuple-element.8, bf16[1,1024,6144]{2,1,0:T(8,128)(2,1)} %all-gather.15.cloned.1.call-done), kind=kOutput, calls=%fused_computation.61 | convolution fusion | flops 25782384640 | bytes 54534144 | tf_op jit(solution)/shard_map/dot_general | solution.py:11
  954.9 6.4 copy.22
  961.3 144.5 %reduce-scatter.17.cloned.1.call-done = bf16[96,1024]{1,0:T(8,128)(2,1)} async-done(((bf16[6144,1024]{1,0:T(8,128)(2,1)}), bf16[96,1024]{1,0:T(8,128)(2,1)}) %reduce-scatter.17.cloned.1.call-update) | async-done | bytes 196624 | tf_op jit(solution)/shard_map/reduce_scatter | solution.py:21
  1107.6 233.0 %reduce-scatter.13.cloned.1.call-done = bf16[16,6144]{1,0:T(8,128)(2,1)} async-done(((bf16[1024,6144]{1,0:T(8,128)(2,1)}), bf16[16,6144]{1,0:T(8,128)(2,1)}) %reduce-scatter.13.cloned.1.call-update) | async-done | bytes 196624 | tf_op jit(solution)/shard_map/reduce_scatter | solution.py:21
  1340.6 234.7 %reduce-scatter.11.cloned.1.call-done = bf16[16,6144]{1,0:T(8,128)(2,1)} async-done(((bf16[1024,6144]{1,0:T(8,128)(2,1)}), bf16[16,6144]{1,0:T(8,128)(2,1)}) %reduce-scatter.11.cloned.1.call-update) | async-done | bytes 196624 | tf_op jit(solution)/shard_map/reduce_scatter | solution.py:21
  1577.1 233.1 %reduce-scatter.9.cloned.1.call-done = bf16[16,6144]{1,0:T(8,128)(2,1)} async-done(((bf16[1024,6144]{1,0:T(8,128)(2,1)}), bf16[16,6144]{1,0:T(8,128)(2,1)}) %reduce-scatter.9.cloned.1.call-update) | async-done | bytes 196624 | tf_op jit(solution)/shard_map/reduce_scatter | solution.py:21
  1810.1 234.6 %reduce-scatter.7.cloned.1.call-done = bf16[16,6144]{1,0:T(8,128)(2,1)} async-done(((bf16[1024,6144]{1,0:T(8,128)(2,1)}), bf16[16,6144]{1,0:T(8,128)(2,1)}) %reduce-scatter.7.cloned.1.call-update) | async-done | bytes 196624 | tf_op jit(solution)/shard_map/reduce_scatter | solution.py:21
  (73 shorter events, 24.8 us)
Async XLA Ops:
  7.2 79.7 %all-gather.15.cloned.1.call-start = ((), (), s32[]{:S(2)}) async-start(), calls=%async_computation.13 | async-start | bytes 12681216 | tf_op jit(solution)/shard_map/all_gather | solution.py:17
  8.9 153.7 %all-gather.17.cloned.1.call-start = ((), (), s32[]{:S(2)}) async-start(), calls=%async_computation.14 | async-start | bytes 12681216 | tf_op jit(solution)/shard_map/all_gather | solution.py:17
  10.7 227.8 %all-gather.19.cloned.1.call-start = ((), (), s32[]{:S(2)}) async-start(), calls=%async_computation.15 | async-start | bytes 12681216 | tf_op jit(solution)/shard_map/all_gather | solution.py:17
  12.5 301.1 %all-gather.21.cloned.1.call-start = ((), (), s32[]{:S(2)}) async-start(), calls=%async_computation.16 | async-start | bytes 12681216 | tf_op jit(solution)/shard_map/all_gather | solution.py:17
  13.3 375.5 %all-gather.23.cloned.1.call-start = ((), (), s32[]{:S(2)}) async-start(), calls=%async_computation.17 | async-start | bytes 12681216 | tf_op jit(solution)/shard_map/all_gather | solution.py:17
  14.0 449.8 %all-gather.13.cloned.1.call-start = ((), (), s32[]{:S(2)}) async-start(), calls=%async_computation.12 | async-start | bytes 12681216 | tf_op jit(solution)/shard_map/all_gather | solution.py:17
  14.7 946.6 %reduce-scatter.15.cloned.1.call-start = ((), (), s32[]{:S(2)}) async-start(), calls=%async_computation.10 | async-start | bytes 12779520 | tf_op jit(solution)/shard_map/reduce_scatter | solution.py:21
  24.2 0.6 copy-start.5
  24.9 137.8 %copy-start.7 = (f32[2048]{0:T(1024)}, f32[2048]{0:T(1024)S(1)}, u32[]{:S(2)}) copy-start(f32[2048]{0:T(1024)S(1)} %add_rsqrt_fusion.1) | copy-start | bytes 24580
  273.7 75.1 %copy-start.13 = (f32[2048]{0:T(1024)}, f32[2048]{0:T(1024)S(1)}, u32[]{:S(2)}) copy-start(f32[2048]{0:T(1024)S(1)} %get-tuple-element.20) | copy-start | bytes 24580
  273.7 115.0 %copy-start.9 = (f32[2048]{0:T(1024)}, f32[2048]{0:T(1024)S(1)}, u32[]{:S(2)}) copy-start(f32[2048]{0:T(1024)S(1)} %add_rsqrt_fusion) | copy-start | bytes 24580
  529.7 34.8 %copy-start.4 = (bf16[2048,1024]{0,1:T(8,128)(2,1)S(1)}, bf16[2048,1024]{0,1:T(8,128)(2,1)}, u32[]{:S(2)}) copy-start(bf16[2048,1024]{0,1:T(8,128)(2,1)} %get-tuple-element.21) | copy-start | bytes 12582916
  564.5 35.2 %copy-start.14 = (f32[2048]{0:T(1024)S(1)}, f32[2048]{0:T(1024)}, u32[]{:S(2)}) copy-start(f32[2048]{0:T(1024)} %copy-done.13) | copy-start | bytes 24580
  564.5 35.2 %copy-start.3 = (bf16[1,2048,1024]{1,2,0:T(8,128)(2,1)S(1)}, bf16[1,2048,1024]{1,2,0:T(8,128)(2,1)}, u32[]{:S(2)}) copy-start(bf16[1,2048,1024]{1,2,0:T(8,128)(2,1)} %copy.9) | copy-start | bytes 12582916
  564.5 35.2 %copy-start.10 = (f32[2048]{0:T(1024)S(1)}, f32[2048]{0:T(1024)}, u32[]{:S(2)}) copy-start(f32[2048]{0:T(1024)} %copy-done.9) | copy-start | bytes 24580
  604.5 2.0 copy-start.1
  638.4 467.3 %reduce-scatter.17.cloned.1.call-start = ((), (), s32[]{:S(2)}) async-start(), calls=%async_computation.11 | async-start | bytes 12779520 | tf_op jit(solution)/shard_map/reduce_scatter | solution.py:21
  681.9 0.7 copy-start.11
  681.9 658.7 %reduce-scatter.13.cloned.1.call-start = ((), (), s32[]{:S(2)}) async-start(), calls=%async_computation.9 | async-start | bytes 12779520 | tf_op jit(solution)/shard_map/reduce_scatter | solution.py:21
  715.4 859.9 %reduce-scatter.11.cloned.1.call-start = ((), (), s32[]{:S(2)}) async-start(), calls=%async_computation.8 | async-start | bytes 12779520 | tf_op jit(solution)/shard_map/reduce_scatter | solution.py:21
  715.4 66.6 %copy-start.8 = (f32[2048]{0:T(1024)S(1)}, f32[2048]{0:T(1024)}, u32[]{:S(2)}) copy-start(f32[2048]{0:T(1024)} %copy-done.7) | copy-start | bytes 24580
  814.6 0.7 copy-start.12
  814.6 995.5 %reduce-scatter.9.cloned.1.call-start = ((), (), s32[]{:S(2)}) async-start(), calls=%async_computation.7 | async-start | bytes 12779520 | tf_op jit(solution)/shard_map/reduce_scatter | solution.py:21
  848.1 1196.6 %reduce-scatter.7.cloned.1.call-start = ((), (), s32[]{:S(2)}) async-start(), calls=%async_computation.6 | async-start | bytes 12779520 | tf_op jit(solution)/shard_map/reduce_scatter | solution.py:21
  880.8 34.7 %copy-start = (bf16[1,2048,1024]{1,2,0:T(8,128)(2,1)S(1)}, bf16[1,2048,1024]{1,2,0:T(8,128)(2,1)}, u32[]{:S(2)}) copy-start(bf16[1,2048,1024]{1,2,0:T(8,128)(2,1)} %copy.10) | copy-start | bytes 12582916
  915.5 34.7 %copy-start.6 = (f32[2048]{0:T(1024)S(1)}, f32[2048]{0:T(1024)}, u32[]{:S(2)}) copy-start(f32[2048]{0:T(1024)} %copy-done.5) | copy-start | bytes 24580
  915.5 34.7 %copy-start.2 = (bf16[2048,1024]{0,1:T(8,128)(2,1)S(1)}, bf16[2048,1024]{0,1:T(8,128)(2,1)}, u32[]{:S(2)}) copy-start(bf16[2048,1024]{0,1:T(8,128)(2,1)} %copy-done.1) | copy-start | bytes 12582916
Sparse Core Ops, SparseCore 0:
  11.6 75.2 all-gather.14
  90.4 72.2 all-gather.16
  166.3 72.2 all-gather.18
  241.4 72.2 all-gather.20
  316.5 72.1 all-gather.22
  391.6 72.1 all-gather.12
  638.6 232.3 reduce-scatter.14
  875.5 230.1 reduce-scatter.16
  1110.4 230.1 reduce-scatter.12
  1345.0 230.1 reduce-scatter.10
  1579.9 230.2 reduce-scatter.8
  1814.6 230.0 reduce-scatter.6

commit v2 on v0

v2 whole, which is shorter than its diff:
```python
import functools

import jax
import jax.numpy as jnp
from jax import lax
from jax.experimental import pallas as pl
from jax.experimental.pallas import tpu as pltpu
from jax.sharding import PartitionSpec as P

BF, F32 = jnp.bfloat16, jnp.float32
MESH = pl.DeviceIdType.MESH
LAYERS = 2
N = 4
STRIDE = (N * N, N, 1)
NN, NT = ((1,), (0,)), ((1,), (1,))
ALL = slice(None)
VMEM_LIMIT = 66 * 1024 * 1024


def dot(a, b, dims=NN):
    return lax.dot_general(a, b, (dims, ((), ())), preferred_element_type=F32)


def place():
    d = lax.axis_index("dp")
    return d // (N * N), lax.rem(d // N, N), lax.rem(d, N)


def along(v, step):
    return lax.rem(v + step + N, N)


def neighbour(axis, step):
    d, v = lax.axis_index("dp"), place()[axis]
    return {"dp": d + (along(v, step) - v) * STRIDE[axis]}


def meet(partner):
    barrier = pltpu.get_barrier_semaphore()
    peers = [neighbour(axis, step) for axis in range(3) for step in (1, -1)]
    if partner:
        peers.append({"rep": 1 - lax.axis_index("rep")})
    for peer in peers:
        pl.semaphore_signal(barrier, inc=1, device_id=peer, device_id_type=MESH)
    pl.semaphore_wait(barrier, len(peers))


class Gather:
    STAGES = 8

    def __init__(self, mine, whole, sems):
        self.mine, self.whole = mine, whole
        self.send, self.recv, self.local = sems

    @staticmethod
    def scratch():
        return [pltpu.SemaphoreType.DMA((9 * 4 + 3 * 4,)), pltpu.SemaphoreType.DMA((9 * 4 + 3 * 4,)), pltpu.SemaphoreType.DMA((3,))]

    def cols(self, c):
        width = self.mine.shape[-1] // 6
        return pl.ds(pl.multiple_of((lax.axis_index("rep") * 3 + c) * width, width), width)

    def chunk(self, p, c, v, h):
        idx = list(place())
        for k in range(p):
            idx[(c + k) % 3] = ALL
        idx[(c + p) % 3] = v
        return self.whole.at[(h, *idx, ALL, self.cols(c))]

    def copy(self, p, c, slot):
        axis = (c + p) % 3
        v = place()[axis]
        own, left, right, far = v, along(v, -1), along(v, 1), along(v, 2)
        both = slice(0, 2)
        sent, h, to = {0: (own, both, 1), 1: (own, both, -1), 2: (left, 0, 1), 3: (right, 1, -1),
                       4: (own, both, 0), 5: (left, both, 0), 6: (right, both, 0), 7: (far, both, 0)}[slot]
        n = (p * 3 + c) * 4 + slot if slot < 4 else 36 + c * 4 + slot - 4
        dst = self.chunk(p, c, sent, h)
        src = self.mine.at[:, :, self.cols(c)] if p == 0 and slot < 2 else dst
        device = neighbour(axis, to) if to else {"rep": 1 - lax.axis_index("rep")}
        return pltpu.make_async_remote_copy(src_ref=src, dst_ref=dst, send_sem=self.send.at[n], recv_sem=self.recv.at[n],
                                            device_id=device, device_id_type=MESH)

    def keep(self, c):
        return pltpu.make_async_copy(self.mine.at[:, :, self.cols(c)], self.whole.at[(ALL, *place(), ALL, self.cols(c))], self.local.at[c])

    def start(self, p, *slots):
        for slot in slots:
            for c in range(3):
                self.copy(p, c, slot).start()

    def wait(self, p, *slots):
        for slot in slots:
            for c in range(3):
                self.copy(p, c, slot).wait_recv()

    def before(self, s):
        p, part = divmod(s - 1, 2)
        if s == 7:
            self.wait(2, 4, 5, 6, 7)
            for p in range(3):
                for slot in range(8 if p == 2 else 4):
                    for c in range(3):
                        self.copy(p, c, slot).wait_send()
        elif s > 0:
            self.wait(p, *((0, 1) if part == 0 else (2, 3)))
            if s == 2:
                for c in range(3):
                    self.keep(c).wait()

    def after(self, s):
        if s == 0:
            self.start(0, 0, 1)
            for c in range(3):
                self.keep(c).start()
        elif s < 7:
            p, part = divmod(s - 1, 2)
            if part == 0:
                self.start(p, 2, 3)
                if p == 2:
                    self.start(2, 5, 6)
            elif p < 2:
                self.start(p + 1, 0, 1)
                if p == 1:
                    self.start(2, 4)
            else:
                self.start(2, 7)


class Scatter:
    STAGES = 7

    def __init__(self, term, out, refs, by_rows):
        self.term, self.out, self.by_rows = term, out, by_rows
        *bufs, self.own, self.part, self.send, self.recv, self.local = refs
        self.bufs = bufs

    @staticmethod
    def scratch(width):
        piece = (16, width)
        return [
            pltpu.VMEM((3, 6, N, N, *piece), BF), pltpu.VMEM((3, 6, N, *piece), BF), pltpu.VMEM((3, 6, *piece), BF),
            pltpu.VMEM((3, 4, N, N, *piece), BF), pltpu.VMEM((3, 2, N, *piece), BF),
            pltpu.SemaphoreType.DMA((54,)), pltpu.SemaphoreType.DMA((54,)), pltpu.SemaphoreType.DMA((12,)),
        ]

    def piece(self, c, h):
        rows, width = self.bufs[0].shape[-2:]
        n = 2 * c + h
        return (slice(n * rows, (n + 1) * rows), ALL) if self.by_rows else (ALL, slice(n * width, (n + 1) * width))

    def value(self, p, c, v, h):
        if p == 0:
            idx = [ALL] * 3
            idx[c] = v
            return self.term.at[(*idx, *self.piece(c, h))]
        if p == 1:
            rest = [k for k in range(3) if k != c]
            idx = [ALL] * 2
            idx[rest.index((c + 1) % 3)] = v
            return self.own.at[(c, 2 + h, *idx)]
        return self.part.at[c, h, v]

    def copy(self, p, c, slot):
        axis = (c + p) % 3
        v = place()[axis]
        at, h, to = {0: (2, 0, 1), 1: (2, 1, -1), 2: (1, 0, 1), 3: (1, 1, 1), 4: (-1, 0, -1), 5: (-1, 1, -1)}[slot]
        buf = self.bufs[p]
        src = buf.at[c, {2: 0, 5: 1}[slot]] if slot in (2, 5) else self.value(p, c, along(v, at), h)
        n = (p * 3 + c) * 6 + slot
        return pltpu.make_async_remote_copy(src_ref=src, dst_ref=buf.at[c, slot], send_sem=self.send.at[n], recv_sem=self.recv.at[n],
                                            device_id=neighbour(axis, to), device_id_type=MESH)

    def load(self, c, k):
        v = place()[c]
        at, h = ((1, 0), (-1, 1), (0, 0), (0, 1))[k]
        return pltpu.make_async_copy(self.value(0, c, along(v, at), h), self.own.at[c, k], self.local.at[c * 4 + k])

    def held(self, p, c, k):
        if p == 0:
            return self.own.at[c, k]
        v = place()[(c + p) % 3]
        at, h = ((1, 0), (-1, 1), (0, 0), (0, 1))[k]
        return self.value(p, c, along(v, at), h)

    @staticmethod
    def add(dst, *srcs):
        def one(i, _):
            at = (i,) if len(dst.shape) > 2 else ()
            total = srcs[0][at].astype(F32) if at else srcs[0][...].astype(F32)
            for src in srcs[1:]:
                total += (src[at] if at else src[...]).astype(F32)
            if at:
                dst[at] = total.astype(BF)
            else:
                dst[...] = total.astype(BF)
            return 0

        if len(dst.shape) > 2:
            lax.fori_loop(0, dst.shape[0], one, 0)
        else:
            one(0, 0)

    def before(self, s):
        if s == 0:
            return
        p, part = divmod(s - 1, 2)
        for c in range(3):
            buf = self.bufs[p]
            if part == 0:
                for k in (0, 1):
                    self.copy(p, c, k).wait_recv()
                    if p == 0:
                        self.load(c, k).wait()
                    self.add(buf.at[c, k], buf.at[c, k], self.held(p, c, k))
            else:
                for slot in (2, 3, 4, 5):
                    self.copy(p, c, slot).wait_recv()
                for h in (0, 1):
                    if p == 0:
                        self.load(c, 2 + h).wait()
                    dst = (self.own.at[c, 2 + h], self.part.at[c, h], self.out.at[self.piece(c, h)])[p]
                    self.add(dst, self.held(p, c, 2 + h), buf.at[c, 2 + h], buf.at[c, 4 + h])
        if s == 6:
            for p in range(3):
                for c in range(3):
                    for slot in range(6):
                        self.copy(p, c, slot).wait_send()

    def after(self, s):
        p, part = divmod(s, 2)
        if p == 3:
            return
        for slot in (0, 1, 3, 4) if part == 0 else (2, 5):
            for c in range(3):
                self.copy(p, c, slot).start()
        if s == 0:
            for k in range(4):
                for c in range(3):
                    self.load(c, k).start()


def run(engine, steps, step, compute):
    last = max(steps) if steps else -1
    groups = {}
    for s, at in enumerate(steps):
        groups.setdefault(at, []).append(s)
    tail = groups[last][1:] if steps and len(groups[last]) > 1 else []
    for at, stages in groups.items():
        @pl.when(step == at)
        def _(first=stages[0]):
            engine.before(first)
    compute()
    for at, stages in groups.items():
        @pl.when(step == at)
        def _(first=stages[0]):
            engine.after(first)
    if tail:
        @pl.when(step == last)
        def _():
            for s in tail:
                engine.before(s)
                engine.after(s)


def params(**more):
    return pltpu.CompilerParams(vmem_limit_bytes=VMEM_LIMIT, **more)


def whole(shape):
    return pl.BlockSpec(shape, lambda *_: (0,) * len(shape), pipeline_mode=pl.Buffered(1))


ANY = pl.BlockSpec(memory_space=pl.ANY)


def gathered(mine, number):
    two, rows, cols = mine.shape

    def kernel(mine, out, *sems):
        meet(True)
        engine = Gather(mine, out, sems)
        for s in range(Gather.STAGES):
            engine.before(s)
            engine.after(s)

    out = pl.pallas_call(
        kernel, out_shape=jax.ShapeDtypeStruct((two, N, N, N, rows, cols), BF), in_specs=[pl.BlockSpec(memory_space=pltpu.VMEM)], out_specs=ANY,
        scratch_shapes=Gather.scratch(), compiler_params=params(collective_id=number, has_side_effects=True), name="gather",
    )(mine)
    return out.reshape(two, -1, cols)


def forward(a, w, mine, number, tile):
    (tokens, d), ff = a.shape, w.shape[-1]
    n = ff // tile
    steps = [round(t * (n - 1) / 23) for t in (0, 2, 4, 7, 10, 19, 23)] + [n - 1]
    rows = min(tokens, 512)

    def kernel(*refs):
        if mine is None:
            a, w, p, q, hid = refs
        else:
            a, w, own, p, q, hid, nxt, *sems = refs
        step = pl.program_id(0)

        def compute():
            def one(i, _):
                r = pl.ds(pl.multiple_of(i * rows, rows), rows)
                gate = dot(a[r, :], w[0])
                up = dot(a[r, :], w[1])
                sig = jax.nn.sigmoid(gate)
                act = gate * sig
                p[r, :] = act
                q[r, :] = up * (sig * (1 + gate * (1 - sig)))
                hid[r, :] = (act * up).astype(BF)
                return 0

            lax.fori_loop(0, tokens // rows, one, 0)

        if mine is None:
            compute()
        else:
            @pl.when(step == 0)
            def _():
                meet(True)

            run(Gather(own, nxt, sems), steps, step, compute)

    block = pl.BlockSpec((tokens, tile), lambda i: (0, i))
    in_specs = [whole((tokens, d)), pl.BlockSpec((2, d, tile), lambda i: (0, 0, i))]
    out_shape = [jax.ShapeDtypeStruct((tokens, ff), t) for t in (F32, F32, BF)]
    out_specs = [block] * 3
    args, more, scratch = [a, w], {}, []
    if mine is not None:
        in_specs.append(whole(mine.shape))
        out_shape.append(jax.ShapeDtypeStruct((2, N, N, N, *mine.shape[1:]), BF))
        out_specs.append(ANY)
        args.append(mine)
        more, scratch = dict(collective_id=number, has_side_effects=True), Gather.scratch()
    outs = pl.pallas_call(
        kernel, grid=(n,), out_shape=out_shape, in_specs=in_specs, out_specs=out_specs, scratch_shapes=scratch, name="forward",
        compiler_params=params(**more),
        cost_estimate=pl.CostEstimate(flops=4 * tokens * d * ff, bytes_accessed=10 * tokens * ff + 4 * d * ff, transcendentals=tokens * ff),
    )(*args)
    return (*outs[:3], outs[3].reshape(2, -1, ff) if mine is not None else None)


def block_of(term):
    return term.reshape(N, N, N, -1, term.shape[-1])


def width_of(term):
    rows, cols = term.shape[-2:]
    return rows * cols // 96


def hidden_backward(g, gt, at, p, q, hid, wd, term, number, tile):
    (tokens, d), ff = g.shape, p.shape[-1]
    n = ff // tile
    steps = [round(t * (n - 1) / 23) for t in (0, 4, 9, 11, 13, 15, 17)]
    rows, cols = min(tokens, 512), min(d, 512)

    def kernel(*refs):
        if term is None:
            g, gt, at, p, q, hid, wd, dgate, dup, dwg, dwu, dwd = refs
        else:
            g, gt, at, p, q, hid, wd, summand, dgate, dup, dwg, dwu, dwd, summed, *scratch = refs
        step = pl.program_id(0)

        def compute():
            def one(i, _):
                r = pl.ds(pl.multiple_of(i * rows, rows), rows)
                dh = dot(g[r, :], wd[...], NT).astype(BF).astype(F32)
                dup[r, :] = (dh * p[r, :]).astype(BF)
                dgate[r, :] = (dh * q[r, :]).astype(BF)
                return 0

            lax.fori_loop(0, tokens // rows, one, 0)

            def two(i, _):
                m = pl.ds(pl.multiple_of(i * cols, cols), cols)
                dwd[:, m] = dot(gt[m, :], hid[...]).astype(BF).T
                dwg[m, :] = dot(at[m, :], dgate[...]).astype(BF)
                dwu[m, :] = dot(at[m, :], dup[...]).astype(BF)
                return 0

            lax.fori_loop(0, d // cols, two, 0)

        if term is None:
            compute()
        else:
            @pl.when(step == 0)
            def _():
                meet(False)

            run(Scatter(summand, summed, scratch, False), steps, step, compute)

    by_col = pl.BlockSpec((tokens, tile), lambda i: (0, i))
    narrow = pl.BlockSpec((d, tile), lambda i: (0, i))
    by_row = pl.BlockSpec((tile, d), lambda i: (i, 0))
    in_specs = [whole((tokens, d)), whole((d, tokens)), whole((d, tokens)), by_col, by_col, by_col, by_row]
    out_shape = [jax.ShapeDtypeStruct(s, BF) for s in ((tokens, ff), (tokens, ff), (d, ff), (d, ff), (ff, d))]
    out_specs = [by_col, by_col, narrow, narrow, by_row]
    args, more, scratch = [g, gt, at, p, q, hid, wd], {}, []
    if term is not None:
        in_specs.append(ANY)
        args.append(block_of(term))
        out_shape.append(jax.ShapeDtypeStruct(args[-1].shape[-2:], BF))
        out_specs.append(whole(args[-1].shape[-2:]))
        more, scratch = dict(collective_id=number, has_side_effects=True), Scatter.scratch(width_of(args[-1]))
    outs = pl.pallas_call(
        kernel, grid=(n,), out_shape=out_shape, in_specs=in_specs, out_specs=out_specs, scratch_shapes=scratch, name="hidden_backward",
        compiler_params=params(**more),
        cost_estimate=pl.CostEstimate(flops=8 * tokens * d * ff, bytes_accessed=14 * tokens * ff + 8 * d * ff, transcendentals=0),
    )(*args)
    return outs if term is not None else (*outs, None)


def input_backward(dgate, dup, w, term, by_rows, number, tile):
    (tokens, ff), d = dgate.shape, w.shape[1]
    n = ff // tile
    steps = [round(t * (n - 1) / 23) for t in (0, 6, 15, 18, 21, 23)] + [n - 1]
    rows = min(tokens, 512)
    term = block_of(term)

    def kernel(dgate, dup, w, summand, out, summed, acc, *scratch):
        step = pl.program_id(0)

        @pl.when(step == 0)
        def _():
            meet(False)

        def compute():
            def one(i, _):
                r = pl.ds(pl.multiple_of(i * rows, rows), rows)
                new = dot(dgate[r, :], w[0], NT) + dot(dup[r, :], w[1], NT)

                @pl.when(step == 0)
                def _():
                    acc[r, :] = new

                @pl.when(step > 0)
                def _():
                    acc[r, :] += new

                return 0

            lax.fori_loop(0, tokens // rows, one, 0)

            @pl.when(step == n - 1)
            def _():
                out[...] = acc[...].astype(BF)

        run(Scatter(summand, summed, scratch, by_rows), steps, step, compute)

    by_col = pl.BlockSpec((tokens, tile), lambda i: (0, i))
    return pl.pallas_call(
        kernel, grid=(n,), out_shape=[jax.ShapeDtypeStruct((tokens, d), BF), jax.ShapeDtypeStruct(term.shape[-2:], BF)],
        in_specs=[by_col, by_col, pl.BlockSpec((2, d, tile), lambda i: (0, 0, i)), ANY],
        out_specs=[whole((tokens, d)), whole(term.shape[-2:])],
        scratch_shapes=[pltpu.VMEM((tokens, d), F32), *Scatter.scratch(width_of(term))], name="input_backward",
        compiler_params=params(collective_id=number, has_side_effects=True),
        cost_estimate=pl.CostEstimate(flops=4 * tokens * d * ff, bytes_accessed=4 * tokens * ff + 4 * d * ff, transcendentals=0),
    )(dgate, dup, w, term)


def scattered(terms, by_rows, number):
    terms = [block_of(t) for t in terms]
    k = len(terms)
    shapes = [Scatter.scratch(width_of(t)) for t in terms]
    size = len(shapes[0])

    def kernel(*refs):
        meet(False)
        engines = [Scatter(refs[j], refs[k + j], refs[2 * k + j * size:2 * k + (j + 1) * size], by_rows[j]) for j in range(k)]
        for s in range(Scatter.STAGES):
            for engine in engines:
                engine.before(s)
                engine.after(s)

    return pl.pallas_call(
        kernel, out_shape=[jax.ShapeDtypeStruct(t.shape[-2:], BF) for t in terms], in_specs=[ANY] * k,
        out_specs=[pl.BlockSpec(memory_space=pltpu.VMEM)] * k, scratch_shapes=sum(shapes, []), name="scatter",
        compiler_params=params(collective_id=number, has_side_effects=True),
    )(*terms)


def scale_of(h):
    wide = h.astype(F32)
    return lax.rsqrt(jnp.mean(wide * wide, -1, keepdims=True) + 1e-6)


def normed(h, s):
    return (h.astype(F32) * s).astype(BF)


def norm_backward(g, h, s, d_a):
    wide, d_a = h.astype(F32), d_a.astype(F32)
    inner = jnp.sum(d_a * wide, -1, keepdims=True) * (s * s * s / h.shape[-1])
    return g + (d_a * s - wide * inner).astype(BF)


def fetch(w):
    half = w.shape[0] // 2
    mine = lax.dynamic_slice_in_dim(w, lax.axis_index("rep") * half, half, 0)
    return lax.all_gather(mine, ("dp", "rep"), axis=0, tiled=True)


def body(tile, x, dy, w_gate, w_up, w_down):
    x, dy = x[0], dy[0]
    mine = [jnp.stack([w_gate[n], w_up[n]]) for n in range(LAYERS)]
    w0 = gathered(mine[0], 1)
    wd0, wd1 = fetch(w_down[0]), fetch(w_down[1])

    s0 = scale_of(x)
    a0 = normed(x, s0)
    p0, q0, hid0, w1 = forward(a0, w0, mine[1], 2, tile)
    h1 = x + dot(hid0, wd0).astype(BF)
    s1 = scale_of(h1)
    a1 = normed(h1, s1)
    p1, q1, hid1, _ = forward(a1, w1, None, None, tile)

    dgate, dup, t_wg1, t_wu1, t_wd1, _ = hidden_backward(dy, dy.T, a1.T, p1, q1, hid1, wd1, None, None, tile)
    g_wd1 = lax.psum_scatter(t_wd1, "dp", scatter_dimension=0, tiled=True)
    d_a, g_wg1 = input_backward(dgate, dup, w1, t_wg1, False, 3, tile)
    g = norm_backward(dy, h1, s1, d_a)

    dgate, dup, t_wg0, t_wu0, t_wd0, g_wu1 = hidden_backward(g, g.T, a0.T, p0, q0, hid0, wd0, t_wu1, 4, tile)
    d_a, g_wd0 = input_backward(dgate, dup, w0, t_wd0, True, 5, tile)
    g_wg0, g_wu0 = scattered([t_wg0, t_wu0], [False, False], 6)
    by_x = norm_backward(g, x, s0, d_a)
    return by_x[None], jnp.stack([g_wg0, g_wg1]), jnp.stack([g_wu0, g_wu1]), jnp.stack([g_wd0, g_wd1])


def solution(mesh):
    seq, row, out = P(("rep", "dp")), P(None, "dp"), P("rep", "dp")
    return jax.shard_map(functools.partial(body, 256), mesh=mesh, in_specs=(seq, seq, row, row, row), out_specs=(seq, out, out, out),
                         check_vma=False)
```

time: 2300 us -> 1010 us (0.44)
  waiting for transfers between devices: 1450 us -> 0.09 us
  Pallas kernels: 0 us -> 881 us
  matrix products: 629 us -> 33.8 us
  other arithmetic: 162 us -> 47.4 us
    unnamed x18 -> x3, waiting for transfers between devices: 1140 us -> 0.07 us
    pallas_call x0 -> x8, Pallas kernels: none -> 881 us  [the longest x2 297 us: hidden_backward(): pl.pallas_call(kernel, grid=(n,), out_shape=out_shape, in_specs=in_specs,...]
    dot_general x17 -> x1, matrix products: 629 us -> 33.8 us  [dot(): return lax.dot_general(a, b, (dims, ((), ())), preferred_element_type=F32)]
    squeeze x6 -> x0, waiting for transfers between devices: 312 us -> none  [stack(): h = layer(h, {name: w[number] for name, w in weights.items()})]
    unnamed x3 -> x0, other arithmetic: 136 us -> none
    transpose x0 -> x4, local copies, waits for them, and re-layouts: none -> 26.1 us  [the longest x2 13.1 us: body(): dgate, dup, t_wg1, t_wu1, t_wd1, _ = hidden_backward(dy, dy.T, a1.T, p1,...]
  transfers between devices with their start and end apart: 12 -> 3, of which waited for: 11 -> 0; matrix products, arithmetic and copies ran while one was open for 27% -> 11% of each run, Pallas kernels for 0% -> 73%
where the time goes in v2:
time: 1010 us
  Pallas kernels  881 us (87%)
  other arithmetic  47.4 us (5%)
  local copies, waits for them, and re-layouts  34.8 us (3%)
  matrix products  33.8 us (3%)
  between operations  13.9 us (1%)
    pallas_call x2, Pallas kernels, hidden_backward(): pl.pallas_call(kernel, grid=(n,), out_shape=out_shape, in_specs=in_specs,...  297 us
    pallas_call x2, Pallas kernels, input_backward(): pl.pallas_call(kernel, grid=(n,), out_shape=[jax.ShapeDtypeStruct((tokens...  214 us
    pallas_call x2, Pallas kernels, forward(): pl.pallas_call(kernel, grid=(n,), out_shape=out_shape, in_specs=in_specs,...  188 us
    pallas_call x1, Pallas kernels, scattered(): pl.pallas_call(kernel, out_shape=[jax.ShapeDtypeStruct(t.shape[-2:], BF)...  98.3 us
    pallas_call x1, Pallas kernels, gathered(): pl.pallas_call(kernel, out_shape=jax.ShapeDtypeStruct((two, N, N, N, rows...  84 us
    dot_general x1, matrix products, dot(): return lax.dot_general(a, b, (dims, ((), ())), preferred_element_type=F32)  33.8 us
  transfers between devices with their start and end apart: 3, of which 0 were waited for; matrix products, arithmetic and copies ran while one was open for 11% of the time, Pallas kernels for 73%

profile of v2, /device:TPU:0, one launch (start us, length us, event | category | flops | bytes accessed | tf_op | source)
XLA Modules:
  0.0 1011.5 jit_solution(15257194071096800469)
XLA Ops:
  7.2 1.0 fusion.18
  9.8 1.1 fusion.19
  10.8 1.1 fusion.20
  11.9 0.9 pad_maximum_fusion
  12.8 84.0 %gather.1 = bf16[2,4,4,4,16,6144]{5,4,3,2,1,0:T(8,128)(2,1)} custom-call(bf16[2,16,6144]{2,1,0:T(8,128)(2,1)} %get-tuple-element.60.mine), custom_call_target="tpu_custom_call" | custom-call | tf_op jit(solution)/shard_map/gather/pallas_call | solution.py:287
  96.8 6.5 copy.10.refs_1_
  103.3 3.1 fusion.4
  107.6 4.9 fusion.5.refs_0_
  112.5 108.9 %forward.2 = (f32[2048,6144]{1,0:T(8,128)}, f32[2048,6144]{1,0:T(8,128)}, bf16[2048,6144]{1,0:T(8,128)(2,1)}, bf16[2,4,4,4,16,6144]{5,4,3,2,1,0:T(8,128)(2,1)}) custom-call(bf16[2048,1024]{1,0:T(8,128)(2,1)} %fusion.5.refs_0_, bf16[2,1024,6144]{2,1,0:T(8,128)(2,1)} %bitcast.40, bf16[2,16,6144]{2,1,0:T(8,128)(2,1)} %get-tuple-element.61.refs_2_), custom_call_target="tpu_custom_call" | custom-call | flops 51539607552 | bytes 150994944 | tf_op jit(solution)/shard_map/forward/pallas_call | solution.py:341
  221.5 33.8 %fusion.7 = (f32[2048]{0:T(1024)S(1)}, bf16[2048,1024]{1,0:T(8,128)(2,1)S(1)}) fusion(bf16[2048,6144]{1,0:T(8,128)(2,1)} %get-tuple-element.28.refs_5_, bf16[1,6144,1024]{2,1,0:T(8,128)(2,1)} %all-gather.5.cloned.1.call-done, bf16[1,2048,1024]{2,1,0:T(8,128)(2,1)} %param.5), kind=kOutput, calls=%fused_computation.17 | convolution fusion | flops 25780287488 | bytes 46145536 | tf_op jit(solution)/shard_map/dot_general | solution.py:21
  255.9 1.4 copy-done.1
  257.3 2.7 fusion.23
  260.0 6.5 copy.11.refs_2_
  266.5 4.9 fusion.8.refs_0_
  271.4 79.4 %forward.3 = (f32[2048,6144]{1,0:T(8,128)}, f32[2048,6144]{1,0:T(8,128)}, bf16[2048,6144]{1,0:T(8,128)(2,1)}) custom-call(bf16[2048,1024]{1,0:T(8,128)(2,1)} %fusion.8.refs_0_, bf16[2,1024,6144]{2,1,0:T(8,128)(2,1)} %bitcast.54), custom_call_target="tpu_custom_call" | custom-call | flops 51539607552 | bytes 150994944 | tf_op jit(solution)/shard_map/forward/pallas_call | solution.py:341
  350.8 143.5 %hidden_backward.2 = (bf16[2048,6144]{1,0:T(8,128)(2,1)}, bf16[2048,6144]{1,0:T(8,128)(2,1)}, bf16[1024,6144]{1,0:T(8,128)(2,1)}, bf16[1024,6144]{1,0:T(8,128)(2,1)}, bf16[6144,1024]{1,0:T(8,128)(2,1)}) custom-call(bf16[2048,1024]{1,0:T(8,128)(2,1)} %bitcast.43, bf16[1024,2048]{1,0:T(8,128)(2,1)} %copy.10.refs_1_, bf16[1024,2048]{1,0:T(8,128)(2,1)} %copy.11.refs_2_, ...), custom_call_target="tpu_custom_call" | custom-call | flops 103079215104 | bytes 226492416 | tf_op jit(solution)/shard_map/hidden_backward/pallas_call | solution.py:412
  495.0 4.9 fusion.22
  499.9 6.5 copy.13.refs_2_
  506.4 107.2 %input_backward.2 = (bf16[2048,1024]{1,0:T(8,128)(2,1)}, bf16[16,6144]{1,0:T(8,128)(2,1)}) custom-call(bf16[2048,6144]{1,0:T(8,128)(2,1)} %get-tuple-element.33.dgate, bf16[2048,6144]{1,0:T(8,128)(2,1)} %get-tuple-element.34.dup, bf16[2,1024,6144]{2,1,0:T(8,128)(2,1)} %bitcast.55, bf16[4,4,4,16,6144]{4,3,2,1,0:T(8,128)(2,1)} %bitcast.57), custom_call_target="tpu_custom_call" | custom-call | flops 51539607552 | bytes 75497472 | tf_op jit(solution)/shard_map/input_backward/pallas_call | solution.py:458
  613.6 4.8 fusion.9
  618.4 0.8 fusion.14
  619.5 5.2 fusion.12.refs_0_
  624.7 6.5 copy.12.refs_1_
  631.2 153.5 %hidden_backward.3 = (bf16[2048,6144]{1,0:T(8,128)(2,1)}, bf16[2048,6144]{1,0:T(8,128)(2,1)}, bf16[1024,6144]{1,0:T(8,128)(2,1)}, bf16[1024,6144]{1,0:T(8,128)(2...) custom-call(bf16[2048,1024]{1,0:T(8,128)(2,1)} %fusion.12.refs_0_, bf16[1024,2048]{1,0:T(8,128)(2,1)} %copy.12.refs_1_, ...), custom_call_target="tpu_custom_call" | custom-call | flops 103079215104 | bytes 226492416 | tf_op jit(solution)/shard_map/hidden_backward/pallas_call | solution.py:412
  784.7 98.3 %scatter.1 = (bf16[16,6144]{1,0:T(8,128)(2,1)}, bf16[16,6144]{1,0:T(8,128)(2,1)}) custom-call(bf16[4,4,4,16,6144]{4,3,2,1,0:T(8,128)(2,1)} %bitcast.44, bf16[4,4,4,16,6144]{4,3,2,1,0:T(8,128)(2,1)} %bitcast.45), custom_call_target="tpu_custom_call" | custom-call | tf_op jit(solution)/shard_map/scatter/pallas_call | solution.py:482
  883.0 106.7 %input_backward.3 = (bf16[2048,1024]{1,0:T(8,128)(2,1)}, bf16[96,1024]{1,0:T(8,128)(2,1)}) custom-call(bf16[2048,6144]{1,0:T(8,128)(2,1)} %get-tuple-element.40.dgate, bf16[2048,6144]{1,0:T(8,128)(2,1)} %get-tuple-element.41.dup, bf16[2,1024,6144]{2,1,0:T(8,128)(2,1)} %bitcast.41, bf16[4,4,4,96,1024]{4,3,2,1,0:T(8,128)(2,1)} %bitcast.58), custom_call_target="tpu_custom_call" | custom-call | flops 51539607552 | bytes 75497472 | tf_op jit(solution)/shard_map/input_backward/pallas_call | solution.py:458
  989.7 4.8 fusion.6
  994.5 1.0 fusion.16
  995.5 1.8 pad_maximum_fusion.3
  997.3 0.8 pad_maximum_fusion.2
  998.1 5.2 fusion.11
  1003.3 1.7 pad_maximum_fusion.4
  (42 shorter events, 4.3 us)
Async XLA Ops:
  7.2 214.3 %all-gather.5.cloned.1.call-start = ((), (), s32[]{:S(2)}) async-start(), calls=%async_computation.2 | async-start | bytes 12681216 | tf_op jit(solution)/shard_map/all_gather | solution.py:507
  8.9 341.9 %all-gather.7.cloned.1.call-start = ((), (), s32[]{:S(2)}) async-start(), calls=%async_computation.3 | async-start | bytes 12681216 | tf_op jit(solution)/shard_map/all_gather | solution.py:507
  9.7 993.6 %reduce-scatter.2.cloned.1.call-start = ((), (), s32[]{:S(2)}) async-start(), calls=%async_computation.1 | async-start | bytes 12779520 | tf_op jit(solution)/shard_map/reduce_scatter | solution.py:525
  106.4 0.6 copy-start.13
  107.0 0.6 copy-start.8
  255.3 0.6 copy-start.14
  255.3 2.0 copy-start.1
  255.9 10.6 %copy-start.11 = (f32[2048]{0:T(1024)}, f32[2048]{0:T(1024)S(1)}, u32[]{:S(2)}) copy-start(f32[2048]{0:T(1024)S(1)} %add_rsqrt_fusion) | copy-start | bytes 24580
  494.3 0.7 copy-start.9
  613.6 5.6 copy-start.2
  613.6 5.9 copy-start.4
  613.6 5.9 copy-start.12
  989.7 7.6 copy-start.5
  989.7 7.6 copy-start.7
  989.7 8.4 copy-start
  989.7 8.4 copy-start.3
  989.7 8.4 copy-start.10
  998.1 5.2 copy-start.6
Sparse Core Ops, SparseCore 0:
  11.6 84.7 all-gather.4
  99.3 82.8 all-gather.6
  494.5 239.0 reduce-scatter.1

commit v3 on v2

v3 whole, which is shorter than its diff:
```python
import functools

import jax
import jax.numpy as jnp
from jax import lax
from jax.experimental import pallas as pl
from jax.experimental.pallas import tpu as pltpu
from jax.sharding import PartitionSpec as P

BF, F32 = jnp.bfloat16, jnp.float32
MESH = pl.DeviceIdType.MESH
LAYERS = 2
N = 4
STRIDE = (N * N, N, 1)
NN, NT = ((1,), (0,)), ((1,), (1,))
ALL = slice(None)
VMEM_LIMIT = 67043328
CHUNK = 512


def dot(a, b, dims=NN):
    return lax.dot_general(a, b, (dims, ((), ())), preferred_element_type=F32)


def place():
    d = lax.axis_index("dp")
    return d // (N * N), lax.rem(d // N, N), lax.rem(d, N)


def along(v, step):
    return lax.rem(v + step + N, N)


def neighbour(axis, step):
    d, v = lax.axis_index("dp"), place()[axis]
    return {"dp": d + (along(v, step) - v) * STRIDE[axis]}


def meet(partner):
    barrier = pltpu.get_barrier_semaphore()
    peers = [neighbour(axis, step) for axis in range(3) for step in (1, -1)]
    if partner:
        peers.append({"rep": 1 - lax.axis_index("rep")})
    for peer in peers:
        pl.semaphore_signal(barrier, inc=1, device_id=peer, device_id_type=MESH)
    pl.semaphore_wait(barrier, len(peers))


class Gather:
    STAGES = 8

    def __init__(self, mine, whole, sems, by_rows=False):
        self.mine, self.whole, self.by_rows = mine, whole, by_rows
        self.send, self.recv, self.local = sems

    @staticmethod
    def scratch():
        return [pltpu.SemaphoreType.DMA((9 * 4 + 3 * 4,)), pltpu.SemaphoreType.DMA((9 * 4 + 3 * 4,)), pltpu.SemaphoreType.DMA((3,))]

    def piece(self, c, h=None):
        n = lax.axis_index("rep") * 3 + c
        rows, cols = self.mine.shape
        if self.by_rows:
            part = ALL if h is None else slice(h * cols // 2, (h + 1) * cols // 2)
            return pl.ds(pl.multiple_of(n * (rows // 6), rows // 6), rows // 6), part
        width = cols // 12
        return ALL, pl.ds(pl.multiple_of((2 * n + (h or 0)) * width, width), 2 * width if h is None else width)

    def chunk(self, p, c, v, h):
        idx = list(place())
        for k in range(p):
            idx[(c + k) % 3] = ALL
        idx[(c + p) % 3] = v
        return self.whole.at[(*idx, *self.piece(c, h))]

    def copy(self, p, c, slot):
        axis = (c + p) % 3
        v = place()[axis]
        own, left, right, far = v, along(v, -1), along(v, 1), along(v, 2)
        sent, h, to = {0: (own, None, 1), 1: (own, None, -1), 2: (left, 0, 1), 3: (right, 1, -1),
                       4: (own, None, 0), 5: (left, None, 0), 6: (right, None, 0), 7: (far, None, 0)}[slot]
        n = (p * 3 + c) * 4 + slot if slot < 4 else 36 + c * 4 + slot - 4
        dst = self.chunk(p, c, sent, h)
        src = self.mine.at[self.piece(c)] if p == 0 and slot < 2 else dst
        device = neighbour(axis, to) if to else {"rep": 1 - lax.axis_index("rep")}
        return pltpu.make_async_remote_copy(src_ref=src, dst_ref=dst, send_sem=self.send.at[n], recv_sem=self.recv.at[n],
                                            device_id=device, device_id_type=MESH)

    def keep(self, c):
        return pltpu.make_async_copy(self.mine.at[self.piece(c)], self.whole.at[(*place(), *self.piece(c))], self.local.at[c])

    def start(self, p, *slots):
        for slot in slots:
            for c in range(3):
                self.copy(p, c, slot).start()

    def wait(self, p, *slots):
        for slot in slots:
            for c in range(3):
                self.copy(p, c, slot).wait_recv()

    def before(self, s):
        p, part = divmod(s - 1, 2)
        if s == 7:
            self.wait(2, 4, 5, 6, 7)
            for p in range(3):
                for slot in range(8 if p == 2 else 4):
                    for c in range(3):
                        self.copy(p, c, slot).wait_send()
        elif s > 0:
            self.wait(p, *((0, 1) if part == 0 else (2, 3)))
            if s == 2:
                for c in range(3):
                    self.keep(c).wait()

    def after(self, s):
        if s == 0:
            self.start(0, 0, 1)
            for c in range(3):
                self.keep(c).start()
        elif s < 7:
            p, part = divmod(s - 1, 2)
            if part == 0:
                self.start(p, 2, 3)
                if p == 2:
                    self.start(2, 5, 6)
            elif p < 2:
                self.start(p + 1, 0, 1)
                if p == 1:
                    self.start(2, 4)
            else:
                self.start(2, 7)


class Scatter:
    STAGES = 7

    def __init__(self, term, out, refs):
        self.term, self.out, self.pair = term, out, len(out.shape) == 3
        *bufs, self.own, self.part, self.send, self.recv, self.local = refs
        self.bufs = bufs

    @staticmethod
    def scratch(width):
        piece = (16, width)
        return [
            pltpu.VMEM((3, 6, N, N, *piece), BF), pltpu.VMEM((3, 6, N, *piece), BF), pltpu.VMEM((3, 6, *piece), BF),
            pltpu.VMEM((3, 4, N, N, *piece), BF), pltpu.VMEM((3, 2, N, *piece), BF),
            pltpu.SemaphoreType.DMA((54,)), pltpu.SemaphoreType.DMA((54,)), pltpu.SemaphoreType.DMA((12,)),
        ]

    def piece(self, c, h, idx=()):
        rows, width = self.bufs[0].shape[-2:]
        if self.pair:
            return h, *idx, ALL, slice(c * width, (c + 1) * width)
        n = 2 * c + h
        return *idx, slice(n * rows, (n + 1) * rows), ALL

    def value(self, p, c, v, h):
        if p == 0:
            idx = [ALL] * 3
            idx[c] = v
            return self.term.at[self.piece(c, h, idx)]
        if p == 1:
            rest = [k for k in range(3) if k != c]
            idx = [ALL] * 2
            idx[rest.index((c + 1) % 3)] = v
            return self.own.at[(c, 2 + h, *idx)]
        return self.part.at[c, h, v]

    def copy(self, p, c, slot):
        axis = (c + p) % 3
        v = place()[axis]
        at, h, to = {0: (2, 0, 1), 1: (2, 1, -1), 2: (1, 0, 1), 3: (1, 1, 1), 4: (-1, 0, -1), 5: (-1, 1, -1)}[slot]
        buf = self.bufs[p]
        src = buf.at[c, {2: 0, 5: 1}[slot]] if slot in (2, 5) else self.value(p, c, along(v, at), h)
        n = (p * 3 + c) * 6 + slot
        return pltpu.make_async_remote_copy(src_ref=src, dst_ref=buf.at[c, slot], send_sem=self.send.at[n], recv_sem=self.recv.at[n],
                                            device_id=neighbour(axis, to), device_id_type=MESH)

    def load(self, c, k):
        v = place()[c]
        at, h = ((1, 0), (-1, 1), (0, 0), (0, 1))[k]
        return pltpu.make_async_copy(self.value(0, c, along(v, at), h), self.own.at[c, k], self.local.at[c * 4 + k])

    def held(self, p, c, k):
        if p == 0:
            return self.own.at[c, k]
        v = place()[(c + p) % 3]
        at, h = ((1, 0), (-1, 1), (0, 0), (0, 1))[k]
        return self.value(p, c, along(v, at), h)

    @staticmethod
    def add(dst, *srcs):
        def one(i, _):
            at = (i,) if len(dst.shape) > 2 else ()
            total = srcs[0][at].astype(F32) if at else srcs[0][...].astype(F32)
            for src in srcs[1:]:
                total += (src[at] if at else src[...]).astype(F32)
            if at:
                dst[at] = total.astype(BF)
            else:
                dst[...] = total.astype(BF)
            return 0

        if len(dst.shape) > 2:
            lax.fori_loop(0, dst.shape[0], one, 0)
        else:
            one(0, 0)

    def before(self, s):
        if s == 0:
            return
        p, part = divmod(s - 1, 2)
        for c in range(3):
            buf = self.bufs[p]
            if part == 0:
                for k in (0, 1):
                    self.copy(p, c, k).wait_recv()
                    if p == 0:
                        self.load(c, k).wait()
                    self.add(buf.at[c, k], buf.at[c, k], self.held(p, c, k))
            else:
                for slot in (2, 3, 4, 5):
                    self.copy(p, c, slot).wait_recv()
                for h in (0, 1):
                    if p == 0:
                        self.load(c, 2 + h).wait()
                    dst = (self.own.at[c, 2 + h], self.part.at[c, h], self.out.at[self.piece(c, h)])[p]
                    self.add(dst, self.held(p, c, 2 + h), buf.at[c, 2 + h], buf.at[c, 4 + h])
        if s == 6:
            for p in range(3):
                for c in range(3):
                    for slot in range(6):
                        self.copy(p, c, slot).wait_send()

    def after(self, s):
        p, part = divmod(s, 2)
        if p == 3:
            return
        for slot in (0, 1, 3, 4) if part == 0 else (2, 5):
            for c in range(3):
                self.copy(p, c, slot).start()
        if s == 0:
            for k in range(4):
                for c in range(3):
                    self.load(c, k).start()


def run(engines, steps, step, last, compute):
    def go(s):
        for engine in engines:
            engine.before(s)
            engine.after(s)

    for s, at in enumerate(steps):
        if at <= last:
            pl.when(step == at)(functools.partial(go, s))
    compute()

    @pl.when(step == last)
    def _():
        for s, at in enumerate(steps):
            if at > last:
                go(s)


def params(**more):
    return pltpu.CompilerParams(vmem_limit_bytes=VMEM_LIMIT, **more)


def whole(shape):
    return pl.BlockSpec(shape, lambda *_: (0,) * len(shape), pipeline_mode=pl.Buffered(1))


ANY = pl.BlockSpec(memory_space=pl.ANY)


def rows_of(tokens):
    size = min(tokens, CHUNK)
    return [pl.ds(i, size) for i in range(0, tokens, size)]


def gathered(wanted, x, number):
    k = len(wanted)

    def kernel(*refs):
        mine, (x, *refs) = refs[:k], refs[k:]
        outs, (a, *sems) = refs[:k], refs[k:]
        meet(True)
        engines = gathers(wanted, mine, outs, sems)
        for s in range(Gather.STAGES):
            for engine in engines:
                engine.before(s)
                engine.after(s)
            if s == 4:
                def one(i, _):
                    r = pl.ds(pl.multiple_of(i * 64, 64), 64)
                    h = x[r, :]
                    a[r, :] = normed(h, scale_of(h))
                    return 0

                lax.fori_loop(0, x.shape[0] // 64, one, 0)

    vmem = pl.BlockSpec(memory_space=pltpu.VMEM)
    arrays, _, shapes, specs, scratch = fetching(wanted)
    *outs, a = pl.pallas_call(
        kernel, out_shape=[*shapes, jax.ShapeDtypeStruct(x.shape, BF)], in_specs=[vmem] * (k + 1), out_specs=[*specs, vmem],
        scratch_shapes=scratch, name="gather", compiler_params=params(collective_id=number, has_side_effects=True),
    )(*arrays, x)
    return *(out.reshape(-1, out.shape[-1]) for out in outs), a


def fetching(wanted):
    arrays = [w for _, w in wanted]
    return (arrays, [whole(w.shape) for w in arrays], [jax.ShapeDtypeStruct((N, N, N, *w.shape[1:]), BF) for w in arrays], [ANY] * len(arrays),
            Gather.scratch() * len(arrays))


def gathers(wanted, mine, outs, sems):
    return [Gather(mine[j].at[n], outs[j], sems[3 * j:3 * j + 3], w.shape[1] > 16) for j, (n, w) in enumerate(wanted)]


def forward(a, wg, wu, flips, wanted, number, tile, steps):
    (tokens, d), ff = a.shape, wg.shape[-1]
    n, k, m = ff // tile, len(flips), len(wanted)
    wide = min(tokens, 128)

    def kernel(*refs):
        a, wg, wu, *refs = refs
        flips, refs = refs[:k], refs[k:]
        own, (p, q, hid, *refs) = refs[:m], refs[m:]
        flipped, refs = refs[:k], refs[k:]
        step = pl.program_id(0)

        def compute():
            for src, dst in zip(flips, flipped):
                r = pl.ds(pl.multiple_of(lax.rem(step, tokens // wide) * wide, wide), wide)
                dst[:, r] = src[r, :].T
            for r in rows_of(tokens):
                gate = dot(a[r, :], wg[...])
                up = dot(a[r, :], wu[...])
                sig = jax.nn.sigmoid(gate)
                act = gate * sig
                p[r, :] = act
                q[r, :] = up * (sig * (1 + gate * (1 - sig)))
                hid[r, :] = (act * up).astype(BF)

        if not wanted:
            compute()
        else:
            @pl.when(step == 0)
            def _():
                meet(True)

            run(gathers(wanted, own, refs[:m], refs[m:]), steps, step, n - 1, compute)

    assert n >= tokens // wide
    block = pl.BlockSpec((tokens, tile), lambda i: (0, i))
    narrow = pl.BlockSpec((d, tile), lambda i: (0, i))
    in_specs = [whole((tokens, d)), narrow, narrow] + [whole((tokens, d))] * k
    out_shape = [jax.ShapeDtypeStruct((tokens, ff), t) for t in (F32, F32, BF)] + [jax.ShapeDtypeStruct((d, tokens), BF)] * k
    out_specs = [block] * 3 + [whole((d, tokens))] * k
    arrays, *new, scratch = fetching(wanted)
    outs = pl.pallas_call(
        kernel, grid=(n,), out_shape=out_shape + new[1], in_specs=in_specs + new[0], out_specs=out_specs + new[2], scratch_shapes=scratch,
        name="forward", compiler_params=params(**(dict(collective_id=number, has_side_effects=True) if wanted else {})),
        cost_estimate=pl.CostEstimate(flops=4 * tokens * d * ff, bytes_accessed=10 * tokens * ff + 4 * d * ff, transcendentals=tokens * ff),
    )(a, wg, wu, *flips, *arrays)
    return (*outs[:3], outs[3:3 + k], [o.reshape(-1, o.shape[-1]) for o in outs[3 + k:]])


def down(hid, wd, h, wanted, number, tile, steps):
    (tokens, ff), d = hid.shape, wd.shape[-1]
    n, m = ff // tile, len(wanted)

    def kernel(hid, wd, h, *refs):
        own, (out, a, *refs) = refs[:m], refs[m:]
        nxt, (acc, *sems) = refs[:m], refs[m:]
        step = pl.program_id(0)

        @pl.when(step == 0)
        def _():
            if wanted:
                meet(True)
            acc[...] = jnp.zeros_like(acc)

        def compute():
            for r in rows_of(tokens):
                acc[r, :] += dot(hid[r, :], wd[...])

            @pl.when(step == n - 1)
            def _():
                def one(i, _):
                    r = pl.ds(pl.multiple_of(i * 64, 64), 64)
                    new = (h[r, :].astype(F32) + acc[r, :].astype(BF).astype(F32)).astype(BF)
                    out[r, :] = new
                    a[r, :] = normed(new, scale_of(new))
                    return 0

                lax.fori_loop(0, tokens // 64, one, 0)

        run(gathers(wanted, own, nxt, sems), steps, step, n - 1, compute)

    in_specs = [pl.BlockSpec((tokens, tile), lambda i: (0, i)), pl.BlockSpec((tile, d), lambda i: (i, 0)), whole((tokens, d))]
    out_shape, out_specs = [jax.ShapeDtypeStruct((tokens, d), BF)] * 2, [whole((tokens, d))] * 2
    arrays, *new, scratch = fetching(wanted)
    outs = pl.pallas_call(
        kernel, grid=(n,), out_shape=out_shape + new[1], in_specs=in_specs + new[0], out_specs=out_specs + new[2],
        scratch_shapes=[pltpu.VMEM((tokens, d), F32), *scratch], name="down",
        compiler_params=params(**(dict(collective_id=number, has_side_effects=True) if wanted else {})),
        cost_estimate=pl.CostEstimate(flops=2 * tokens * d * ff, bytes_accessed=2 * tokens * ff + 2 * d * ff, transcendentals=0),
    )(hid, wd, h, *arrays)
    return (*outs[:2], [o.reshape(-1, o.shape[-1]) for o in outs[2:]])


def block_of(term):
    return term.reshape(*term.shape[:-2], N, N, N, -1, term.shape[-1])


def shape_of(term):
    return term.shape[:-5] + term.shape[-2:]


def buffers(terms):
    return sum((Scatter.scratch(t.shape[-1] // (3 if t.ndim == 6 else 1)) for t in terms), [])


def traffic(ins, outs, scratch):
    size = len(scratch) // max(len(ins), 1)
    return [Scatter(ins[j], outs[j], scratch[j * size:(j + 1) * size]) for j in range(len(ins))]


def hidden_backward(g, gt, at, p, q, hid, wd, span, into, terms, number, tile, steps):
    (tokens, d), ff = g.shape, p.shape[-1]
    first, n = span
    k, m = len(terms), len(into)
    cols = min(d, 512)

    def kernel(g, gt, at, p, q, hid, wd, *refs):
        summands, refs = refs[m:m + k], refs[m + k:]
        dgate, dup, dwd, dw, *refs = refs
        summed, scratch = refs[:k], refs[k:]
        step = pl.program_id(0)

        def compute():
            for r in rows_of(tokens):
                dh = dot(g[r, :], wd[...], NT).astype(BF).astype(F32)
                dup[r, :] = (dh * p[r, :]).astype(BF)
                dgate[r, :] = (dh * q[r, :]).astype(BF)
            for i in range(0, d, cols):
                r = pl.ds(i, cols)
                dwd[:, r] = dot(gt[r, :], hid[...]).astype(BF).T
            for i in range(0, d, cols):
                r = pl.ds(i, cols)
                dw[0, r, :] = dot(at[r, :], dgate[...]).astype(BF)
                dw[1, r, :] = dot(at[r, :], dup[...]).astype(BF)

        if not terms:
            compute()
        else:
            @pl.when(step == 0)
            def _():
                meet(False)

            run(traffic(summands, summed, scratch), steps, step, n - 1, compute)

    by_col = pl.BlockSpec((tokens, tile), lambda i: (0, i + first))
    both = pl.BlockSpec((2, d, tile), lambda i: (0, 0, i))
    by_row = pl.BlockSpec((tile, d), lambda i: (i + first, 0))
    terms = [block_of(t) for t in terms]
    shapes = [shape_of(t) for t in terms]
    return pl.pallas_call(
        kernel, grid=(n,), name="hidden_backward",
        out_shape=[jax.ShapeDtypeStruct(s, BF) for s in ((tokens, ff), (tokens, ff), (ff, d), (2, d, n * tile), *shapes)],
        in_specs=[whole((tokens, d)), whole((d, tokens)), whole((d, tokens)), by_col, by_col, by_col, by_row] + [ANY] * (m + k),
        out_specs=[by_col, by_col, by_row, both] + [whole(s) for s in shapes],
        scratch_shapes=buffers(terms), input_output_aliases={7 + j: j for j in range(m)},
        compiler_params=params(**(dict(collective_id=number, has_side_effects=True) if terms else {})),
        cost_estimate=pl.CostEstimate(flops=8 * tokens * d * n * tile, bytes_accessed=(14 * tokens + 8 * d) * n * tile, transcendentals=0),
    )(g, gt, at, p, q, hid, wd, *into, *terms)


def input_backward(dgate, dup, wg, wu, h, g, terms, number, tile, steps):
    (tokens, ff), d = dgate.shape, wg.shape[0]
    n, k = ff // tile, len(terms)
    size = min(tokens, 256)
    terms = [block_of(t) for t in terms]

    def kernel(dgate, dup, wg, wu, h, g, *refs):
        summands, (out, *refs) = refs[:k], refs[k:]
        summed, (acc, held, sems, *scratch) = refs[:k], refs[k:]
        step = pl.program_id(0)

        @pl.when(step == 0)
        def _():
            if terms:
                meet(False)
            acc[...] = jnp.zeros_like(acc)

        def loads(i):
            r, slot = pl.ds(pl.multiple_of(i * size, size), size), lax.rem(i, 2)
            return [pltpu.make_async_copy(src.at[r, :], held.at[slot, j], sems.at[slot, j]) for j, src in enumerate((h, g))]

        def finish(i, _):
            @pl.when(i + 1 < tokens // size)
            def _():
                for load in loads(i + 1):
                    load.start()

            for load in loads(i):
                load.wait()

            def one(j, _):
                q = pl.ds(pl.multiple_of(j * 64, 64), 64)
                r = pl.ds(pl.multiple_of(i * size + j * 64, 64), 64)
                old, by_new = held[lax.rem(i, 2), 0, q, :], held[lax.rem(i, 2), 1, q, :]
                out[r, :] = norm_backward(by_new, old, scale_of(old), acc[r, :].astype(BF))
                return 0

            lax.fori_loop(0, size // 64, one, 0)
            return 0

        def compute():
            for r in rows_of(tokens):
                acc[r, :] += dot(dgate[r, :], wg[...], NT) + dot(dup[r, :], wu[...], NT)

            @pl.when(step == n - 1)
            def _():
                for load in loads(0):
                    load.start()
                lax.fori_loop(0, tokens // size, finish, 0)

        run(traffic(summands, summed, scratch), steps, step, n - 1, compute)

    by_col = pl.BlockSpec((tokens, tile), lambda i: (0, i))
    narrow = pl.BlockSpec((d, tile), lambda i: (0, i))
    shapes = [shape_of(t) for t in terms]
    return pl.pallas_call(
        kernel, grid=(n,), out_shape=[jax.ShapeDtypeStruct(s, BF) for s in ((tokens, d), *shapes)],
        in_specs=[by_col, by_col, narrow, narrow] + [ANY] * (2 + k),
        out_specs=[whole((tokens, d))] + [whole(s) for s in shapes], name="input_backward",
        scratch_shapes=[pltpu.VMEM((tokens, d), F32), pltpu.VMEM((2, 2, size, d), BF), pltpu.SemaphoreType.DMA((2, 2))]
        + buffers(terms),
        compiler_params=params(**(dict(collective_id=number, has_side_effects=True) if terms else {})),
        cost_estimate=pl.CostEstimate(flops=4 * tokens * d * ff, bytes_accessed=4 * tokens * ff + 4 * d * ff, transcendentals=0),
    )(dgate, dup, wg, wu, h, g, *terms)


def scale_of(h):
    wide = h.astype(F32)
    return lax.rsqrt(jnp.mean(wide * wide, -1, keepdims=True) + 1e-6)


def normed(h, s):
    return (h.astype(F32) * s).astype(BF)


def norm_backward(g, h, s, d_a):
    wide, d_a = h.astype(F32), d_a.astype(F32)
    inner = jnp.sum(d_a * wide, -1, keepdims=True) * (s * s * s / h.shape[-1])
    return (g.astype(F32) + (d_a * s - wide * inner).astype(BF).astype(F32)).astype(BF)


def body(x, dy, w_gate, w_up, w_down):
    x, dy = x[0], dy[0]
    tiles = w_gate.shape[-1] // 256
    first, second = (0, tiles // 2), (tiles // 2, tiles - tiles // 2)
    one, two = (0, 3, 7, 8, 10, 11, 12), (0, 15, 24, 24, 24, 24, 24)

    wg0, wu0, a0 = gathered([(0, w_gate), (0, w_up)], x, 1)
    p0, q0, hid0, (at0,), (wd0, wg1) = forward(a0, wg0, wu0, [a0], [(0, w_down), (1, w_gate)], 2, 256, (0, 2, 4, 6, 9, 19, 23, 24))
    h1, a1, (wu1,) = down(hid0, wd0, x, [(1, w_up)], 3, 512, (0, 2, 3, 5, 7, 12, 12, 12))
    p1, q1, hid1, (at1, dyt), (wd1,) = forward(a1, wg1, wu1, [a1, dy], [(1, w_down)], 4, 256, (0, 2, 5, 8, 11, 18, 21, 23))

    *some, t1a = hidden_backward(dy, dyt, at1, p1, q1, hid1, wd1, first, (), [], None, 256, ())
    dgate, dup, t_wd1, t1b, g1a = hidden_backward(dy, dyt, at1, p1, q1, hid1, wd1, second, some, [t1a], 5, 256, one)
    g, g_wd1 = input_backward(dgate, dup, wg1, wu1, h1, dy, [t_wd1], 6, 512, one)

    gt = g.T
    *some, t0a, g1b = hidden_backward(g, gt, at0, p0, q0, hid0, wd0, first, (), [t1b], 7, 256, one)
    dgate, dup, t_wd0, t0b, g0a = hidden_backward(g, gt, at0, p0, q0, hid0, wd0, second, some, [t0a], 8, 256, one)
    by_x, g_wd0, g0b = input_backward(dgate, dup, wg0, wu0, x, g, [t_wd0, t0b], 9, 256, two)

    by_gate, by_up = jnp.stack([jnp.concatenate([g0a, g0b], -1), jnp.concatenate([g1a, g1b], -1)], 1)
    return by_x[None], by_gate, by_up, jnp.stack([g_wd0, g_wd1])


def solution(mesh):
    seq, row, out = P(("rep", "dp")), P(None, "dp"), P("rep", "dp")
    return jax.shard_map(body, mesh=mesh, in_specs=(seq, seq, row, row, row), out_specs=(seq, out, out, out),
                         check_vma=False)
```

time: 1010 us -> 770 us (0.76); the launches traced: 1010 us -> 761 us
  Pallas kernels: 881 us -> 745 us
  other arithmetic: 47.4 us -> 4.02 us
  matrix products: 33.8 us -> 0 us
  local copies, waits for them, and re-layouts: 34.8 us -> 11.1 us
  between operations: 13.9 us -> 0.89 us
    pallas_call x8 -> x10, Pallas kernels: 881 us -> 745 us  [the longest x4 285 us: hidden_backward(): pl.pallas_call(kernel, grid=(n,), name='hidden_backward', out_shape=[jax....]
    dot_general x1 -> x0, matrix products: 33.8 us -> none  [dot(): return lax.dot_general(a, b, (dims, ((), ())), preferred_element_type=F32)]
    transpose x4 -> x0, local copies, waits for them, and re-layouts: 26.1 us -> none  [the longest x2 13.1 us: body(): dgate, dup, t_wg1, t_wu1, t_wd1, _ = hidden_backward(dy, dy.T, a1.T, p1,...]
    reduce_sum x3 -> x0, other arithmetic: 12.6 us -> none  [the longest x2 9.51 us: norm_backward(): inner = jnp.sum(d_a * wide, -1, keepdims=True) * (s * s * s / h.shape[-1])]
  transfers between devices with their start and end apart: 3 -> 0, of which waited for: 0 -> 0; matrix products, arithmetic and copies ran while one was open for 11% -> 0% of each run, Pallas kernels for 73% -> 0%
where the time goes in v3:
time: 770 us; the launch traced here: 761 us
  Pallas kernels  745 us (97%)
  local copies, waits for them, and re-layouts  11.1 us (1%)
    pallas_call x4, Pallas kernels, hidden_backward(): pl.pallas_call(kernel, grid=(n,), name='hidden_backward', out_shape=[jax....  285 us
    pallas_call x2, Pallas kernels, input_backward(): pl.pallas_call(kernel, grid=(n,), out_shape=[jax.ShapeDtypeStruct(s, BF)...  180 us
    pallas_call x2, Pallas kernels, forward(): pl.pallas_call(kernel, grid=(n,), out_shape=out_shape + new[1], in_specs=...  159 us
    pallas_call x1, Pallas kernels, gathered(): pl.pallas_call(kernel, out_shape=[*shapes, jax.ShapeDtypeStruct(x.shape,...  66 us
    pallas_call x1, Pallas kernels, down(): pl.pallas_call(kernel, grid=(n,), out_shape=out_shape + new[1], in_specs=...  55.2 us

profile of v3, /device:TPU:0, one launch (start us, length us, event | category | flops | bytes accessed | tf_op | source)
XLA Modules:
  0.0 761.0 jit_solution(4646925272495606179)
XLA Ops:
  0.6 66.0 %gather.1 = (bf16[4,4,4,16,6144]{4,3,2,1,0:T(8,128)(2,1)}, bf16[4,4,4,16,6144]{4,3,2,1,0:T(8,128)(2,1)}, bf16[2048,1024]{1,0:T(8,128)(2,1)}) custom-call(bf16[2,16,6144]{2,1,0:T(8,128)(2,1)} %refs_5_.2, bf16[2,16,6144]{2,1,0:T(8,128)(2,1)} %refs_0_.3, bf16[2048,1024]{1,0:T(8,128)(2,1)} %bitcast.41), custom_call_target="tpu_custom_call" | custom-call | tf_op jit(solution)/shard_map/gather/pallas_call | solution.py:307
  66.6 82.0 %forward.2 = (f32[2048,6144]{1,0:T(8,128)}, f32[2048,6144]{1,0:T(8,128)}, bf16[2048,6144]{1,0:T(8,128)(2,1)}, bf16[1024,2048]{1,0:T(8,128)(2,1)}, bf16[4,4,4,96,...) custom-call(bf16[2048,1024]{1,0:T(8,128)(2,1)} %get-tuple-element.46.refs_0_.refs_3_, ...), custom_call_target="tpu_custom_call" | custom-call | flops 51539607552 | bytes 150994944 | tf_op jit(solution)/shard_map/forward/pallas_call | solution.py:365
  148.6 55.2 %down.1 = (bf16[2048,1024]{1,0:T(8,128)(2,1)}, bf16[2048,1024]{1,0:T(8,128)(2,1)}, bf16[4,4,4,16,6144]{4,3,2,1,0:T(8,128)(2,1)}) custom-call(bf16[2048,6144]{1,0:T(8,128)(2,1)} %get-tuple-element.49.hid, bf16[6144,1024]{1,0:T(8,128)(2,1)} %bitcast.28, bf16[2048,1024]{1,0:T(8,128)(2,1)} %bitcast.42, bf16[2,16,6144]{2,1,0:T(8,128)(2,1)} %refs_0_.3), custom_call_target="tpu_custom_call" | custom-call | flops 25769803776 | bytes 37748736 | tf_op jit(solution)/shard_map/down/pallas_call | solution.py:408
  203.7 76.6 %forward.3 = (f32[2048,6144]{1,0:T(8,128)}, f32[2048,6144]{1,0:T(8,128)}, bf16[2048,6144]{1,0:T(8,128)(2,1)}, bf16[1024,2048]{1,0:T(8,128)(2,1)}, bf16[1024,2048...) custom-call(bf16[2048,1024]{1,0:T(8,128)(2,1)} %get-tuple-element.51.refs_0_.refs_3_, bf16[1024,6144]{1,0:T(8,128)(2,1)} %bitcast.53, ...), custom_call_target="tpu_custom_call" | custom-call | flops 51539607552 | bytes 150994944 | tf_op jit(solution)/shard_map/forward/pallas_call | solution.py:365
  280.4 65.1 %hidden_backward.4 = (bf16[2048,6144]{1,0:T(8,128)(2,1)}, bf16[2048,6144]{1,0:T(8,128)(2,1)}, bf16[6144,1024]{1,0:T(8,128)(2,1)}, bf16[2,1024,3072]{2,1,0:T(8,128)(2,1)}) custom-call(bf16[2048,1024]{1,0:T(8,128)(2,1)} %bitcast.38, bf16[1024,2048]{1,0:T(8,128)(2,1)} %get-tuple-element.54.gt, bf16[1024,2048]{1,0:T(8,128)(2,1)} %get-tuple-element.55.at, ...), custom_call_target="tpu_custom_call" | custom-call | flops 51539607552 | bytes 113246208 | tf_op jit(solution)/shard_map/hidden_backward/pallas_call | solution.py:473
  345.4 75.0 %hidden_backward.5 = (bf16[2048,6144]{1,0:T(8,128)(2,1)}, bf16[2048,6144]{1,0:T(8,128)(2,1)}, bf16[6144,1024]{1,0:T(8,128)(2,1)}, bf16[2,1024,3072]{2,1,0:T(8,128)(2,1)}, bf16[2,16,3072]{2,1,0:T(8,128)(2,1)}) custom-call(bf16[2048,1024]{1,0:T(8,128)(2,1)} %bitcast.39, ...), custom_call_target="tpu_custom_call", output_to_operand_aliasing={{0}: (7, {}), {1}: (8, {}), {2}: (9, {})} | custom-call | flops 51539607552 | bytes 113246208 | tf_op jit(solution)/shard_map/hidden_backward/pallas_call | solution.py:473
  420.4 76.0 %input_backward.2 = (bf16[2048,1024]{1,0:T(8,128)(2,1)}, bf16[96,1024]{1,0:T(8,128)(2,1)}) custom-call(bf16[2048,6144]{1,0:T(8,128)(2,1)} %get-tuple-element.64.dgate, bf16[2048,6144]{1,0:T(8,128)(2,1)} %get-tuple-element.65.dup, bf16[1024,6144]{1,0:T(8,128)(2,1)} %bitcast.54, bf16[1024,6144]{1,0:T(8,128)(2,1)} %bitcast.56, ...), custom_call_target="tpu_custom_call" | custom-call | flops 51539607552 | bytes 75497472 | tf_op jit(solution)/shard_map/input_backward/pallas_call | solution.py:539
  496.4 6.4 copy.15
  502.8 72.3 %hidden_backward.6 = (bf16[2048,6144]{1,0:T(8,128)(2,1)}, bf16[2048,6144]{1,0:T(8,128)(2,1)}, bf16[6144,1024]{1,0:T(8,128)(2,1)}, bf16[2,1024,3072]{2,1,0:T(8,128)(2,1)}, bf16[2,16,3072]{2,1,0:T(8,128)(2,1)}) custom-call(bf16[2048,1024]{1,0:T(8,128)(2,1)} %get-tuple-element.68.g, bf16[1024,2048]{1,0:T(8,128)(2,1)} %bitcast.26, ...), custom_call_target="tpu_custom_call" | custom-call | flops 51539607552 | bytes 113246208 | tf_op jit(solution)/shard_map/hidden_backward/pallas_call | solution.py:473
  575.1 72.7 %hidden_backward.7 = (bf16[2048,6144]{1,0:T(8,128)(2,1)}, bf16[2048,6144]{1,0:T(8,128)(2,1)}, bf16[6144,1024]{1,0:T(8,128)(2,1)}, bf16[2,1024,3072]{2,1,0:T(8,128)(2,1)}, bf16[2,16,3072]{2,1,0:T(8,128)(2,1)}) custom-call(bf16[2048,1024]{1,0:T(8,128)(2,1)} %get-tuple-element.68.g, ...), custom_call_target="tpu_custom_call", output_to_operand_aliasing={{0}: (7, {}), {1}: (8, {}), {2}: (9, {})} | custom-call | flops 51539607552 | bytes 113246208 | tf_op jit(solution)/shard_map/hidden_backward/pallas_call | solution.py:473
  647.9 104.2 %input_backward.3 = (bf16[2048,1024]{1,0:T(8,128)(2,1)}, bf16[96,1024]{1,0:T(8,128)(2,1)}, bf16[2,16,3072]{2,1,0:T(8,128)(2,1)}) custom-call(bf16[2048,6144]{1,0:T(8,128)(2,1)} %get-tuple-element.77.dgate, bf16[2048,6144]{1,0:T(8,128)(2,1)} %get-tuple-element.78.dup, bf16[1024,6144]{1,0:T(8,128)(2,1)} %bitcast.48, bf16[1024,6144]{1,0:T(8,128)(2,1)} %bitcast.50, ...), custom_call_target="tpu_custom_call" | custom-call | flops 51539607552 | bytes 75497472 | tf_op jit(solution)/shard_map/input_backward/pallas_call | solution.py:539
  752.1 1.8 pad_maximum_fusion.1
  753.9 1.3 maximum_bitcast_fusion
  755.2 0.9 fusion.2
  756.2 4.6 copy.23
